TPU v7x, 32 devices: a whole 2x2x4 slice. The times are simulated.
32 devices in a mesh: dp: 32 (over z, y, x, core).
Axes of the slice: x: 2, y: 2, z: 4, core: 2. Of those that a mesh axis runs over, the one named last changes fastest.
Arguments:
- x_in: bfloat16 [32768, 1024], P('dp')
- dy_mid: bfloat16 [32768, 4096], P('dp')
- x_mid: bfloat16 [32768, 4096], P('dp')
- dy_out: bfloat16 [32768, 1024], P('dp')
- w_fc1: float32 [1024, 4096], replicated
- w_fc2: float32 [4096, 1024], replicated
- stat_left: float32 [32, 512, 512], P('dp')
- stat_right: float32 [32, 512, 512], P('dp')
- root_left: float32 [32, 512, 512], P('dp')
- root_right: float32 [32, 512, 512], P('dp')
- graft_sq: float32 [32, 512, 512], P('dp')
- momentum: float32 [32, 512, 512], P('dp')
Outputs:
- output 1: float32 [1024, 4096], replicated
- output 2: float32 [4096, 1024], replicated
- output 3: float32 [32, 512, 512], P('dp')
- output 4: float32 [32, 512, 512], P('dp')
- output 5: float32 [32, 512, 512], P('dp')
- output 6: float32 [32, 512, 512], P('dp')
All inputs are finite; a program needn't handle non-finite values.
Results may differ from a plain program's by a relative error of at most 0.001.
Values are sent between devices in bfloat16 or wider.
A program may use at most 1 GiB of HBM per device.

v0:
```python
import jax
import jax.numpy as jnp
from jax import lax
from jax.sharding import PartitionSpec as P

STEP = 10
STAT_DECAY = 0.999
MOM_DECAY = 0.9
GRAFT_EPS = 1e-8
LEARN_RATE = 0.01
WEIGHT_DECAY = 1e-4
BIAS_CORR = 1.0 - STAT_DECAY ** STEP


def grad_blocks(x_rows, dy_rows, block_dim):
    n_tok, n_in = x_rows.shape
    n_out = dy_rows.shape[1]
    in_blocks = -(-n_in // block_dim)
    out_blocks = -(-n_out // block_dim)
    x_pad = jnp.pad(x_rows, ((0, 0), (0, in_blocks * block_dim - n_in))).reshape(n_tok, in_blocks, block_dim)
    dy_pad = jnp.pad(dy_rows, ((0, 0), (0, out_blocks * block_dim - n_out))).reshape(n_tok, out_blocks, block_dim)
    grad_tiles = jnp.einsum('tri,tcj->rcij', x_pad, dy_pad, preferred_element_type=jnp.float32)
    return grad_tiles.reshape(in_blocks * out_blocks, block_dim, block_dim)


def from_blocks(dir_blocks, n_rows, n_cols):
    block_dim = dir_blocks.shape[-1]
    row_blocks = -(-n_rows // block_dim)
    col_blocks = -(-n_cols // block_dim)
    full_mat = dir_blocks.reshape(row_blocks, col_blocks, block_dim, block_dim).transpose(0, 2, 1, 3)
    return full_mat.reshape(row_blocks * block_dim, col_blocks * block_dim)[:n_rows, :n_cols]


def keep_mask(block_ids, n_model, n_hidden, block_dim):
    model_blocks = -(-n_model // block_dim)
    hidden_blocks = -(-n_hidden // block_dim)
    half_count = model_blocks * hidden_blocks
    is_first = block_ids < half_count
    local_ids = block_ids % half_count
    row_first = jnp.minimum(n_model - (local_ids // hidden_blocks) * block_dim, block_dim)
    col_first = jnp.minimum(n_hidden - (local_ids % hidden_blocks) * block_dim, block_dim)
    row_second = jnp.minimum(n_hidden - (local_ids // model_blocks) * block_dim, block_dim)
    col_second = jnp.minimum(n_model - (local_ids % model_blocks) * block_dim, block_dim)
    row_count = jnp.where(is_first, row_first, row_second)
    col_count = jnp.where(is_first, col_first, col_second)
    offsets = jnp.arange(block_dim)
    return (offsets[None, :, None] < row_count[:, None, None]) & (offsets[None, None, :] < col_count[:, None, None])


def stat_update(grad_blk, stat_left, stat_right):
    left_prod = jnp.einsum('nik,njk->nij', grad_blk, grad_blk, precision=lax.Precision.HIGHEST, preferred_element_type=jnp.float32)
    right_prod = jnp.einsum('nki,nkj->nij', grad_blk, grad_blk, precision=lax.Precision.HIGHEST, preferred_element_type=jnp.float32)
    return STAT_DECAY * stat_left + (1.0 - STAT_DECAY) * left_prod, STAT_DECAY * stat_right + (1.0 - STAT_DECAY) * right_prod


def direction_update(grad_blk, root_left, root_right, graft_sq, momentum, keep_tiles):
    left_mul = jnp.einsum('nij,njk->nik', root_left, grad_blk, precision=lax.Precision.HIGHEST, preferred_element_type=jnp.float32)
    precond = jnp.einsum('nij,njk->nik', left_mul, root_right, precision=lax.Precision.HIGHEST, preferred_element_type=jnp.float32)
    precond = jnp.where(keep_tiles, precond, 0.0)
    new_sq = STAT_DECAY * graft_sq + (1.0 - STAT_DECAY) * grad_blk * grad_blk
    graft_dir = grad_blk / (jnp.sqrt(new_sq / BIAS_CORR) + GRAFT_EPS)
    graft_norm = jnp.sqrt(jnp.sum(graft_dir * graft_dir, axis=(1, 2)))
    pre_norm = jnp.sqrt(jnp.sum(precond * precond, axis=(1, 2)))
    new_mom = MOM_DECAY * momentum + precond * (graft_norm / pre_norm)[:, None, None]
    return new_sq, new_mom


def apply_update(w_fc1, w_fc2, dir_blocks):
    n_model, n_hidden = w_fc1.shape
    half_count = dir_blocks.shape[0] // 2
    dir_fc1 = from_blocks(dir_blocks[:half_count], n_model, n_hidden)
    dir_fc2 = from_blocks(dir_blocks[half_count:], n_hidden, n_model)
    new_w1 = w_fc1 - LEARN_RATE * (dir_fc1.astype(jnp.float32) + WEIGHT_DECAY * w_fc1)
    new_w2 = w_fc2 - LEARN_RATE * (dir_fc2.astype(jnp.float32) + WEIGHT_DECAY * w_fc2)
    return new_w1, new_w2


def solution(mesh):
    n_dev = mesh.shape['dp']

    def per_device(x_in, dy_mid, x_mid, dy_out, w_fc1, w_fc2, stat_left, stat_right, root_left, root_right, graft_sq, momentum):
        block_dim = stat_left.shape[-1]
        n_model, n_hidden = w_fc1.shape
        own_count = stat_left.shape[0]
        local_grad = jnp.concatenate([grad_blocks(x_in, dy_mid, block_dim), grad_blocks(x_mid, dy_out, block_dim)], axis=0)
        own_grad = lax.psum_scatter(local_grad, 'dp', scatter_dimension=0, tiled=True) / n_dev
        block_ids = lax.axis_index('dp') * own_count + jnp.arange(own_count)
        keep_tiles = keep_mask(block_ids, n_model, n_hidden, block_dim)
        new_left, new_right = stat_update(own_grad, stat_left, stat_right)
        new_sq, new_mom = direction_update(own_grad, root_left, root_right, graft_sq, momentum, keep_tiles)
        all_dir = lax.all_gather(new_mom.astype(jnp.bfloat16), 'dp', axis=0, tiled=True)
        new_w1, new_w2 = apply_update(w_fc1, w_fc2, all_dir)
        return new_w1, new_w2, new_left, new_right, new_sq, new_mom

    row_spec = P('dp', None)
    rep_spec = P(None, None)
    tile_spec = P('dp', None, None)
    in_specs = (row_spec, row_spec, row_spec, row_spec, rep_spec, rep_spec, tile_spec, tile_spec, tile_spec, tile_spec, tile_spec, tile_spec)
    out_specs = (rep_spec, rep_spec, tile_spec, tile_spec, tile_spec, tile_spec)
    return jax.shard_map(per_device, mesh=mesh, in_specs=in_specs, out_specs=out_specs, check_vma=False)
```

profile of v0, /device:TPU:0, one launch (start us, length us, event | category | flops | bytes accessed | tf_op | source)
XLA Modules:
  0.0 756.0 jit_solution(5313523920344410280)
XLA Ops:
  7.2 0.0 copy-start
  7.2 0.0 reduce-scatter.2.cloned.1.call-start
  7.2 2.9 copy.43
  10.2 14.6 %fusion.2 = f32[8,2,512,512]{2,3,0,1:T(8,128)} fusion(bf16[1024,2,512,1]{0,2,3,1:T(8,128)(2,1)S(1)} %bitcast.91, bf16[128,8,8,512]{3,2,1,0:T(8,128)(2,1)} %bitcast.92), kind=kOutput, calls=%fused_computation.9 | convolution fusion | flops 8589934592 | bytes 27262976 | tf_op jit(solution)/shard_map/tri,tcj->rcij/dot_general | solution.py:22
  24.8 17.3 %copy.37 = f32[8,2,512,512]{3,2,1,0:T(8,128)} copy(f32[8,2,512,512]{2,3,0,1:T(8,128)} %fusion.2) | data formatting | bytes 33554432 | tf_op jit(solution)/shard_map/tri,tcj->rcij/transpose | solution.py:22
  42.1 0.0 copy-start.4
  42.1 12.1 %copy.42 = bf16[1024,4096]{0,1:T(8,128)(2,1)} copy(bf16[1024,4096]{1,0:T(8,128)(2,1)} %param.13) | data formatting | bytes 16777216 | tf_op jit(solution)/shard_map/reshape | solution.py:21
  54.3 0.0 copy-done.4
  54.3 14.7 %convolution_bitcast_fusion = f32[2,8,512,512]{2,3,0,1:T(8,128)} fusion(bf16[1024,8,512,1]{0,2,3,1:T(8,128)(2,1)} %bitcast.90, bf16[128,2,8,512]{3,2,1,0:T(8,128)(2,1)S(1)} %bitcast.93), kind=kOutput, calls=%fused_computation.5 | convolution fusion | flops 8589934592 | bytes 27262976 | tf_op jit(solution)/shard_map/tri,tcj->rcij/dot_general | solution.py:22
  68.9 17.5 %copy.34 = f32[2,8,512,512]{3,2,1,0:T(8,128)} copy(f32[2,8,512,512]{2,3,0,1:T(8,128)} %convolution_bitcast_fusion) | data formatting | bytes 33554432 | tf_op jit(solution)/shard_map/tri,tcj->rcij/transpose | solution.py:22
  86.5 24.0 %pad_maximum_fusion = f32[32,512,512]{2,1,0:T(8,128)} fusion(f32[16,512,512]{2,1,0:T(8,128)} %bitcast.86, f32[16,512,512]{2,1,0:T(8,128)} %bitcast.87), kind=kLoop, calls=%fused_computation | loop fusion | flops 8388608 | bytes 67108864 | tf_op jit(solution)/shard_map/concatenate | solution.py:85
  110.5 0.0 copy-start.3
  110.5 0.0 reduce-scatter.2.cloned.1.call-update
  110.5 0.2 all-gather.2.cloned.1.call-start
  110.9 357.0 %reduce-scatter.2.cloned.1.call-done = f32[1,512,512]{2,1,0:T(8,128)} async-done(((f32[32,512,512]{2,1,0:T(8,128)}), f32[1,512,512]{2,1,0:T(8,128)}) %reduce-scatter.2.cloned.1.call-update) | async-done | bytes 1048592 | tf_op jit(solution)/shard_map/reduce_scatter | solution.py:86
  467.8 0.0 copy-start.2
  467.8 3.8 multiply_reduce_fusion.1
  472.3 0.0 copy-done.3
  472.3 4.7 fusion.9
  477.1 0.0 copy-done
  477.1 2.7 multiply_reduce_fusion
  480.4 2.6 fusion.23
  483.0 0.0 all-gather.2.cloned.1.call-update
  483.1 4.7 fusion.6
  487.8 0.0 copy-done.2
  487.8 4.1 fusion.7
  492.0 112.9 %all-gather.2.cloned.1.call-done = bf16[32,512,512]{2,1,0:T(8,128)(2,1)} async-done(((bf16[1,512,512]{2,1,0:T(8,128)(2,1)}), bf16[32,512,512]{2,1,0:T(8,128)(2,1)}) %all-gather.2.cloned.1.call-update) | async-done | bytes 16777232 | tf_op jit(solution)/shard_map/all_gather | solution.py:91
  604.9 11.6 %fusion.24 = (bf16[16,512,512]{2,1,0:T(8,128)(2,1)}, bf16[16,512,512]{2,1,0:T(8,128)(2,1)}) fusion(bf16[32,512,512]{2,1,0:T(8,128)(2,1)} %all-gather.2.cloned.1.call-done), kind=kLoop, calls=%fused_computation.41 | loop fusion | bytes 33554432 | tf_op jit(solution)/shard_map/slice | solution.py:72
  616.5 11.8 %convert_bitcast_fusion.1 = f32[2,512,8,512]{3,1,2,0:T(8,128)} fusion(bf16[2,8,512,512]{3,2,1,0:T(8,128)(2,1)} %bitcast.89), kind=kLoop, calls=%fused_computation.2 | loop fusion | flops 4194304 | bytes 25165824 | tf_op jit(solution)/shard_map/convert_element_type | solution.py:73
  628.4 15.2 %copy.38 = f32[2,512,8,512]{3,2,1,0:T(8,128)S(1)} copy(f32[2,512,8,512]{3,1,2,0:T(8,128)} %convert_bitcast_fusion.1) | data formatting | bytes 33554432 | tf_op jit(solution)/shard_map/convert_element_type | solution.py:73
  643.6 19.1 %copy.46 = f32[128,8,8,512]{3,1,2,0:T(8,128)} copy(f32[128,8,8,512]{3,2,1,0:T(8,128)S(1)} %bitcast.84) | data formatting | bytes 33554432
  662.8 11.8 %convert_bitcast_fusion = f32[8,512,2,512]{3,1,2,0:T(8,128)} fusion(bf16[8,2,512,512]{3,2,1,0:T(8,128)(2,1)} %bitcast.88), kind=kLoop, calls=%fused_computation.1 | loop fusion | flops 4194304 | bytes 25165824 | tf_op jit(solution)/shard_map/convert_element_type | solution.py:74
  674.6 0.0 slice-start
  674.6 0.0 slice-start.1
  674.6 29.1 %copy.39 = f32[8,512,2,512]{3,2,1,0:T(2,128)} copy(f32[8,512,2,512]{3,1,2,0:T(8,128)} %convert_bitcast_fusion) | data formatting | bytes 33554432 | tf_op jit(solution)/shard_map/convert_element_type | solution.py:74
  703.7 0.0 slice-start.2
  703.7 0.0 slice-start.3
  703.7 15.0 %copy.47 = f32[512,8,2,512]{3,1,2,0:T(8,128)} copy(f32[512,8,2,512]{3,2,1,0:T(2,128)} %bitcast.85) | data formatting | bytes 33554432
  718.7 0.0 slice-done
  718.7 0.0 slice-done.1
  718.7 0.0 slice-done.2
  718.7 0.0 slice-done.3
  718.7 12.5 %multiply_subtract_fusion.1 = f32[1024,4096]{1,0:T(8,128)} fusion(f32[1024,4096]{1,0:T(8,128)} %param.16, f32[1024,4096]{1,0:T(8,128)S(1)} %bitcast.82), kind=kLoop, calls=%fused_computation.4 | loop fusion | flops 16777216 | bytes 50331648 | tf_op jit(solution)/shard_map/sub | solution.py:73
  731.2 0.0 copy-start.1
  731.2 17.5 %multiply_subtract_fusion = f32[4096,1024]{1,0:T(8,128)} fusion(f32[4096,1024]{1,0:T(8,128)} %param.17, f32[4096,1024]{1,0:T(8,128)} %bitcast.83), kind=kLoop, calls=%fused_computation.3 | loop fusion | flops 16777216 | bytes 50331648 | tf_op jit(solution)/shard_map/sub | solution.py:74
  748.7 0.0 copy-done.1
  (2 shorter events, 0.0 us)
Async XLA Ops:
  7.2 469.9 %copy-start = (f32[1,512,512]{2,1,0:T(8,128)S(1)}, f32[1,512,512]{2,1,0:T(8,128)}, u32[]{:S(2)}) copy-start(f32[1,512,512]{2,1,0:T(8,128)} %param.21) | copy-start | bytes 3145732
  7.2 460.6 %reduce-scatter.2.cloned.1.call-start = ((), (), s32[]{:S(2)}) async-start(), calls=%async_computation.1 | async-start | bytes 34603008 | tf_op jit(solution)/shard_map/reduce_scatter | solution.py:86
  42.1 12.2 %copy-start.4 = (bf16[1024,1024]{1,0:T(8,128)(2,1)S(1)}, bf16[1024,1024]{1,0:T(8,128)(2,1)}, u32[]{:S(2)}) copy-start(bf16[1024,1024]{1,0:T(8,128)(2,1)} %param.12) | copy-start | bytes 6291460
  110.5 361.8 %copy-start.3 = (f32[1,512,512]{2,1,0:T(8,128)S(1)}, f32[1,512,512]{2,1,0:T(8,128)}, u32[]{:S(2)}) copy-start(f32[1,512,512]{2,1,0:T(8,128)} %param.20) | copy-start | bytes 3145732
  110.5 494.3 %all-gather.2.cloned.1.call-start = ((), (), s32[]{:S(2)}) async-start(), calls=%async_computation.2 | async-start | bytes 17301504 | tf_op jit(solution)/shard_map/all_gather | solution.py:91
  467.8 20.0 %copy-start.2 = (f32[1,512,512]{2,1,0:T(8,128)S(1)}, f32[1,512,512]{2,1,0:T(8,128)}, u32[]{:S(2)}) copy-start(f32[1,512,512]{2,1,0:T(8,128)} %reduce-scatter.2.cloned.1.call-done) | copy-start | bytes 3145732
  674.6 44.1 %slice-start = ((s8[16777216]{0:T(1024)(128)(4,1)}), s8[4194304]{0:T(1024)(128)(4,1)S(1)}, s32[]{:S(2)}) async-start(s8[16777216]{0:T(1024)(128)(4,1)} %bitcast.80), calls=%async_computation.3 | async-start | bytes 8388608
  674.6 44.1 %slice-start.1 = ((s8[16777216]{0:T(1024)(128)(4,1)}), s8[4194304]{0:T(1024)(128)(4,1)S(1)}, s32[]{:S(2)}) async-start(s8[16777216]{0:T(1024)(128)(4,1)} %bitcast.80), calls=%async_computation.4 | async-start | bytes 8388608
  703.7 15.0 %slice-start.2 = ((s8[16777216]{0:T(1024)(128)(4,1)}), s8[4194304]{0:T(1024)(128)(4,1)S(1)}, s32[]{:S(2)}) async-start(s8[16777216]{0:T(1024)(128)(4,1)} %bitcast.80), calls=%async_computation.5 | async-start | bytes 8388608
  703.7 15.0 %slice-start.3 = ((s8[16777216]{0:T(1024)(128)(4,1)}), s8[4194304]{0:T(1024)(128)(4,1)S(1)}, s32[]{:S(2)}) async-start(s8[16777216]{0:T(1024)(128)(4,1)} %bitcast.80), calls=%async_computation.6 | async-start | bytes 8388608
  731.2 17.5 %copy-start.1 = (f32[1,512,512]{2,1,0:T(8,128)S(1)}, f32[1,512,512]{2,1,0:T(8,128)}, u32[]{:S(2)}) copy-start(f32[1,512,512]{2,1,0:T(8,128)} %param.21) | copy-start | bytes 3145732
Sparse Core Ops, SparseCore 0:
  110.7 357.1 reduce-scatter.1
  483.2 121.6 all-gather.1
where the time goes:
time: 764 us; the launch traced here: 756 us
  waiting for transfers between devices  470 us (62%)
  local copies, waits for them, and re-layouts  140 us (18%)
  other arithmetic  84.2 us (11%)
  matrix products  45.5 us (6%)
  between operations  16 us (2%)
    reduce_scatter x1, waiting for transfers between devices, per_device(): lax.psum_scatter(local_grad, 'dp', scatter_dimension=0, tiled=True) / n_dev  357 us
    all_gather x1, waiting for transfers between devices, per_device(): lax.all_gather(new_mom.astype(jnp.bfloat16), 'dp', axis=0, tiled=True)  113 us
    transpose x2, local copies, waits for them, and re-layouts, grad_blocks(): jnp.einsum('tri,tcj->rcij', x_pad, dy_pad, preferred_element_type=jnp.flo...  34.9 us
    unnamed x20, local copies, waits for them, and re-layouts  34.2 us
    dot_general x2, matrix products, grad_blocks(): jnp.einsum('tri,tcj->rcij', x_pad, dy_pad, preferred_element_type=jnp.flo...  29.3 us
    convert_element_type x1, local copies, waits for them, and re-layouts, apply_update(): dir_fc2.astype(jnp.float32) + WEIGHT_DECAY * w_fc2  29.1 us
    concatenate x1, other arithmetic, per_device(): jnp.concatenate([grad_blocks(x_in, dy_mid, block_dim), grad_blocks(x_mid,...  24 us
    sub x1, other arithmetic, apply_update(): w_fc2 - LEARN_RATE * (dir_fc2.astype(jnp.float32) + WEIGHT_DECAY * w_fc2)  17.5 us
  transfers between devices with their start and end apart: 2, of which 2 were waited for; matrix products, arithmetic and copies ran while one was open for 1% of the time, Pallas kernels for 0%

commit v1 on v0

v1 whole, which is shorter than its diff:
```python
import functools

import jax
import jax.numpy as jnp
from jax import lax
from jax.experimental import pallas as pl
from jax.experimental.pallas import tpu as pltpu
from jax.sharding import PartitionSpec as P

STEP = 10
STAT_DECAY = 0.999
MOM_DECAY = 0.9
GRAFT_EPS = 1e-8
LEARN_RATE = 0.01
WEIGHT_DECAY = 1e-4
BIAS_CORR = 1.0 - STAT_DECAY ** STEP

MESH = pl.DeviceIdType.MESH
HOPS = (2, 3, 1, 0)
GATHER_HOPS = (0, 1, 3, 2)


def dev(z, y, x, c):
    return (((z * 2 + y) * 2 + x) * 2 + c,)


def coords():
    me = lax.axis_index("dp")
    return me // 8, (me // 4) % 2, (me // 2) % 2, me % 2


def greet(z, y, x, c):
    barrier = pltpu.get_barrier_semaphore()
    peers = [dev(z, y, 1 - x, c), dev(z, 1 - y, x, c), dev(z, y, x, 1 - c)]
    peers += [dev((z + k) % 4, y, x, c) for k in (1, 2, 3)]
    for peer in peers:
        pl.semaphore_signal(barrier, inc=1, device_id=peer, device_id_type=MESH)
    pl.semaphore_wait(barrier, len(peers))


def remote(src, dst, send_sem, recv_sem, peer):
    return pltpu.make_async_remote_copy(src_ref=src, dst_ref=dst, send_sem=send_sem, recv_sem=recv_sem, device_id=peer, device_id_type=MESH)


def reduce_kernel(x_in, dy_mid, x_mid, dy_out, out_ref, xi, dm, xm, do, acc, rx, ry, rz, lsem, psem, qsem, xs, xr, ys, yr, zs, zr, osem):
    z, y, x, c = coords()
    rows = x_in.shape[0]
    bd = 512
    half = bd // 2
    xp, yp, cp = dev(z, y, 1 - x, c), dev(z, 1 - y, x, c), dev(z, y, x, 1 - c)
    own = y * 2 + x

    def cols(i):
        return pl.ds(pl.multiple_of(i * bd, bd), bd)

    def operand(kind, i):
        if kind == "xi":
            return i, x_in.at[:, cols(i)], x_in.at[:, cols(i)], xi.at[i]
        if kind == "dm":
            return 2 + i, dy_mid.at[:, cols(2 * i + c)], dy_mid.at[:, cols(2 * i + 1 - c)], dm.at[i]
        if kind == "xm":
            return 6 + i, x_mid.at[:, cols(i)], x_mid.at[:, cols(i)], xm.at[i]
        return 14, dy_out.at[:, cols(c)], dy_out.at[:, cols(1 - c)], do

    def here(kind, i):
        s, mine, _, dst = operand(kind, i)
        return pltpu.make_async_copy(mine, dst.at[pl.ds(0, rows)], lsem.at[s])

    def there(kind, i):
        s, _, theirs, dst = operand(kind, i)
        return remote(theirs, dst.at[pl.ds(rows, rows)], qsem.at[s], psem.at[s], cp)

    def fetch(kind, i):
        there(kind, i).start()
        here(kind, i).start()

    def arrive(kind, i):
        here(kind, i).wait()
        there(kind, i).wait_recv()

    greet(z, y, x, c)

    zb = [(z + h) % 4 for h in HOPS]
    first1 = [zb[0] < 2, (zb[1] < 2) & (zb[0] >= 2)]
    first2 = [zb[0] >= 2, (zb[1] >= 2) & (zb[0] < 2)]
    first1 += [(zb[2] < 2) & (zb[0] >= 2) & (zb[1] >= 2), zb[0] < 0]
    first2 += [(zb[2] >= 2) & (zb[0] < 2) & (zb[1] < 2), zb[0] < 0]
    order = [(1 - y) * 2 + 1 - x, y * 2 + 1 - x, (1 - y) * 2 + x, own]

    for k in range(4):
        @pl.when(zb[k] < 2)
        def _():
            fetch("xi", zb[k])

        @pl.when(first2[k])
        def _():
            fetch("do", 0)

        for q in range(4):
            @pl.when(first1[k])
            def _():
                fetch("dm", order[q])

            @pl.when(zb[k] >= 2)
            def _():
                fetch("xm", (zb[k] - 2) * 4 + order[q])

    def dots(lhs, rhs, dst):
        for h in range(2):
            dst[h] = lax.dot_general(lhs[:, h * half:(h + 1) * half], rhs[...], (((0,), (0,)), ((), ())), preferred_element_type=jnp.float32)

    def send_one(k, q, j):
        @pl.when(q < 2)
        def _():
            remote(acc.at[k, j, 0], rx.at[k, q], xs.at[k, q], xr.at[k, q], xp).start()

        @pl.when(q % 2 == 0)
        def _():
            remote(acc.at[k, j, 1], ry.at[k, q // 2], ys.at[k, q // 2], yr.at[k, q // 2], yp).start()

    def pick(values, i):
        out = values[-1]
        for n in range(len(values) - 2, -1, -1):
            out = jnp.where(i == n, values[n], out)
        return out

    def group(k, _):
        zk = pick(zb, k)
        f1, f2 = pick([v.astype(jnp.int32) for v in first1], k), pick([v.astype(jnp.int32) for v in first2], k)

        @pl.when(zk < 2)
        def _():
            arrive("xi", zk)

        @pl.when(f2 == 1)
        def _():
            arrive("do", 0)

        def tile(q, _):
            j = pick(order, q)

            @pl.when(f1 == 1)
            def _():
                arrive("dm", j)

            @pl.when(zk < 2)
            def _():
                dots(xi.at[zk], dm.at[j], acc.at[k, j])

            @pl.when(zk >= 2)
            def _():
                t = (zk - 2) * 4 + j
                arrive("xm", t)
                dots(xm.at[t], do, acc.at[k, j])

            @pl.when(k < 2)
            def _():
                send_one(k, q, j)

            return 0

        return lax.fori_loop(0, 4, tile, 0)

    lax.fori_loop(0, 4, group, 0)

    def add(k, j, h, ref):
        acc[k, j, h] += ref[...]

    def got(buf, ss, rs, k, i):
        remote(buf.at[k, i], buf.at[k, i], ss.at[k, i], rs.at[k, i], xp).wait_recv()

    def start_one(k):
        for q in range(3):
            if q < 2:
                remote(acc.at[k, order[q], 0], rx.at[k, q], xs.at[k, q], xr.at[k, q], xp).start()
            if q % 2 == 0:
                remote(acc.at[k, order[q], 1], ry.at[k, q // 2], ys.at[k, q // 2], yr.at[k, q // 2], yp).start()

    def start_two(k):
        got(rx, xs, xr, k, 0)
        add(k, order[2], 0, rx.at[k, 0])
        remote(acc.at[k, order[2], 0], ry.at[k, 2], ys.at[k, 2], yr.at[k, 2], yp).start()
        got(ry, ys, yr, k, 0)
        add(k, order[1], 1, ry.at[k, 0])
        remote(acc.at[k, order[1], 1], rx.at[k, 2], xs.at[k, 2], xr.at[k, 2], xp).start()

    def finish_plane(k):
        got(rx, xs, xr, k, 1)
        add(k, own, 0, rx.at[k, 1])
        got(ry, ys, yr, k, 1)
        add(k, own, 1, ry.at[k, 1])
        for h, (buf, ss, rs) in enumerate(((ry, ys, yr), (rx, xs, xr))):
            got(buf, ss, rs, k, 2)
            add(k, own, h, buf.at[k, 2])
            if k < 3:
                remote(acc.at[k, own, h], rz.at[k, h], zs.at[k, h], zr.at[k, h], dev(zb[k], y, x, c)).start()

    start_two(0)
    start_one(2)
    start_two(1)
    finish_plane(0)
    start_two(2)
    start_one(3)
    finish_plane(1)
    finish_plane(2)
    start_two(3)
    finish_plane(3)

    for k in range(3):
        for h in range(2):
            remote(rz.at[k, h], rz.at[k, h], zs.at[k, h], zr.at[k, h], xp).wait_recv()
            add(3, own, h, rz.at[k, h])
    outs = []
    for h in range(2):
        acc[3, own, h] = acc[3, own, h] * (1.0 / 32.0)
        o = pltpu.make_async_copy(acc.at[3, own, h], out_ref.at[pl.ds(h * half, half)], osem.at[h])
        o.start()
        outs.append(o)
    for s in range(15):
        kind, i = ("xi", s) if s < 2 else ("dm", s - 2) if s < 6 else ("xm", s - 6) if s < 14 else ("do", 0)
        there(kind, i).wait_send()
    for k in range(4):
        for i in range(3):
            remote(rx.at[k, i], rx.at[k, i], xs.at[k, i], xr.at[k, i], xp).wait_send()
            remote(ry.at[k, i], ry.at[k, i], ys.at[k, i], yr.at[k, i], yp).wait_send()
    for k in range(3):
        for h in range(2):
            remote(rz.at[k, h], rz.at[k, h], zs.at[k, h], zr.at[k, h], xp).wait_send()
    for o in outs:
        o.wait()


def reduce_gradients(x_in, dy_mid, x_mid, dy_out):
    bf, f32 = jnp.bfloat16, jnp.float32
    rows = 2 * x_in.shape[0]
    dma = pltpu.SemaphoreType.DMA
    any_spec = pl.BlockSpec(memory_space=pl.ANY)
    return pl.pallas_call(
        reduce_kernel,
        out_shape=jax.ShapeDtypeStruct((512, 512), f32),
        in_specs=[any_spec] * 4,
        out_specs=any_spec,
        scratch_shapes=[
            pltpu.VMEM((2, rows, 512), bf), pltpu.VMEM((4, rows, 512), bf), pltpu.VMEM((8, rows, 512), bf), pltpu.VMEM((rows, 512), bf),
            pltpu.VMEM((4, 4, 2, 256, 512), f32), pltpu.VMEM((4, 3, 256, 512), f32), pltpu.VMEM((4, 3, 256, 512), f32), pltpu.VMEM((3, 2, 256, 512), f32),
            dma((15,)), dma((15,)), dma((15,)), dma((4, 3)), dma((4, 3)), dma((4, 3)), dma((4, 3)), dma((3, 2)), dma((3, 2)), dma((2,)),
        ],
        compiler_params=pltpu.CompilerParams(collective_id=0, has_side_effects=True, vmem_limit_bytes=67043328),
        name="reduce",
    )(x_in, dy_mid, x_mid, dy_out)


def gather_kernel(dir_ref, d1, d2, buf, isem, zs, zr, xs, xr, ys, yr, xds, xdr, yds, ydr, cs, cr, osem):
    z, y, x, c = coords()
    xp, yp, cp = dev(z, y, 1 - x, c), dev(z, 1 - y, x, c), dev(z, y, x, 1 - c)

    def blk(zb, yb, xb, cb):
        return dev(zb, yb, xb, cb)[0]

    bring = pltpu.make_async_copy(dir_ref, buf.at[blk(z, y, x, c)], isem)
    bring.start()
    greet(z, y, x, c)
    bring.wait()

    zb = [(z + 4 - h) % 4 for h in GATHER_HOPS]
    spots = [(y, x), (1 - y, x), (y, 1 - x), (1 - y, 1 - x)]

    def put(b, zk, n):
        def one():
            return pltpu.make_async_copy(buf.at[b], d1.at[pl.ds(pl.multiple_of((b // 8) * 512, 512), 512), pl.ds(pl.multiple_of((b % 8) * 512, 512), 512)], osem.at[n])

        def two():
            return pltpu.make_async_copy(buf.at[b], d2.at[pl.ds(pl.multiple_of(((b - 16) // 2) * 512, 512), 512), pl.ds(pl.multiple_of((b % 2) * 512, 512), 512)], osem.at[n])

        @pl.when(zk < 2)
        def _():
            one().start()

        @pl.when(zk >= 2)
        def _():
            two().start()

    def whole(ref, b):
        return ref.at[b]

    def part(ref, b, h):
        return ref.at[b, pl.ds(h * 256, 256)]

    def xcopy(k, b):
        return remote(buf.at[b], buf.at[b], xs.at[k], xr.at[k], xp)

    def ycopy(k, b):
        return remote(buf.at[b], buf.at[b], ys.at[k], yr.at[k], yp)

    def xdiag(k, b):
        return remote(part(buf, b, 0), part(buf, b, 0), xds.at[k], xdr.at[k], xp)

    def ydiag(k, b):
        return remote(part(buf, b, 1), part(buf, b, 1), yds.at[k], ydr.at[k], yp)

    def ccopy(k, i, b):
        return remote(buf.at[b], buf.at[b], cs.at[k, i], cr.at[k, i], cp)

    def zcopy(k, b, peer):
        return remote(buf.at[b], buf.at[b], zs.at[k - 1], zr.at[k - 1], peer)

    def open_group(k):
        b = blk(zb[k], y, x, c)
        xcopy(k, b).start()
        ycopy(k, b).start()
        ccopy(k, 0, b).start()
        put(b, zb[k], k * 8)

    b0 = blk(z, y, x, c)
    xcopy(0, b0).start()
    ycopy(0, b0).start()
    for k in (1, 2, 3):
        zcopy(k, b0, dev((z + GATHER_HOPS[k]) % 4, y, x, c)).start()
    ccopy(0, 0, b0).start()
    put(b0, z, 0)
    for k in range(4):
        by, bx, bd = [blk(zb[k], yy, xx, c) for yy, xx in spots[1:]]
        ycopy(k, by).wait_recv()
        xdiag(k, by).start()
        ccopy(k, 1, by).start()
        put(by, zb[k], k * 8 + 1)
        xcopy(k, bx).wait_recv()
        ydiag(k, bx).start()
        ccopy(k, 2, bx).start()
        put(bx, zb[k], k * 8 + 2)
        if k < 3:
            zcopy(k + 1, blk(zb[k + 1], y, x, c), xp).wait_recv()
            open_group(k + 1)
        xdiag(k, bd).wait_recv()
        ydiag(k, bd).wait_recv()
        ccopy(k, 3, bd).start()
        put(bd, zb[k], k * 8 + 3)
        for i, (yy, xx) in enumerate(spots):
            bo = blk(zb[k], yy, xx, 1 - c)
            ccopy(k, i, bo).wait_recv()
            put(bo, zb[k], k * 8 + 4 + i)
    for k in range(4):
        xcopy(k, b0).wait_send()
        ycopy(k, b0).wait_send()
        xdiag(k, b0).wait_send()
        ydiag(k, b0).wait_send()
        for i in range(4):
            ccopy(k, i, b0).wait_send()
        if k:
            zcopy(k, b0, xp).wait_send()
    for n in range(32):
        pltpu.make_async_copy(buf.at[0], d1.at[pl.ds(0, 512), pl.ds(0, 512)], osem.at[n]).wait()


def gather_directions(own_dir):
    bf = jnp.bfloat16
    dma = pltpu.SemaphoreType.DMA
    any_spec = pl.BlockSpec(memory_space=pl.ANY)
    return pl.pallas_call(
        gather_kernel,
        out_shape=(jax.ShapeDtypeStruct((1024, 4096), bf), jax.ShapeDtypeStruct((4096, 1024), bf)),
        in_specs=[any_spec],
        out_specs=(any_spec, any_spec),
        scratch_shapes=[pltpu.VMEM((32, 512, 512), bf), dma, dma((3,)), dma((3,))] + [dma((4,))] * 8 + [dma((4, 4)), dma((4, 4)), dma((32,))],
        compiler_params=pltpu.CompilerParams(collective_id=1, has_side_effects=True, vmem_limit_bytes=40 * 2 ** 20),
        name="gather",
    )(own_dir)


def mm(a, b):
    return jnp.dot(a, b, precision=lax.Precision.HIGHEST, preferred_element_type=jnp.float32)


def solution(mesh):
    def per_device(x_in, dy_mid, x_mid, dy_out, w_fc1, w_fc2, stat_left, stat_right, root_left, root_right, graft_sq, momentum):
        grad = reduce_gradients(x_in, dy_mid, x_mid, dy_out)
        precond = mm(mm(root_left[0], grad), root_right[0])
        new_sq = STAT_DECAY * graft_sq[0] + (1.0 - STAT_DECAY) * grad * grad
        graft_dir = grad / (jnp.sqrt(new_sq / BIAS_CORR) + GRAFT_EPS)
        graft_norm = jnp.sqrt(jnp.sum(graft_dir * graft_dir))
        pre_norm = jnp.sqrt(jnp.sum(precond * precond))
        new_mom = MOM_DECAY * momentum[0] + precond * (graft_norm / pre_norm)
        dir1, dir2 = gather_directions(new_mom.astype(jnp.bfloat16))
        new_left = STAT_DECAY * stat_left[0] + (1.0 - STAT_DECAY) * mm(grad, grad.T)
        new_right = STAT_DECAY * stat_right[0] + (1.0 - STAT_DECAY) * mm(grad.T, grad)
        new_w1 = w_fc1 - LEARN_RATE * (dir1.astype(jnp.float32) + WEIGHT_DECAY * w_fc1)
        new_w2 = w_fc2 - LEARN_RATE * (dir2.astype(jnp.float32) + WEIGHT_DECAY * w_fc2)
        return new_w1, new_w2, new_left[None], new_right[None], new_sq[None], new_mom[None]

    row_spec = P('dp', None)
    rep_spec = P(None, None)
    tile_spec = P('dp', None, None)
    in_specs = (row_spec, row_spec, row_spec, row_spec, rep_spec, rep_spec, tile_spec, tile_spec, tile_spec, tile_spec, tile_spec, tile_spec)
    out_specs = (rep_spec, rep_spec, tile_spec, tile_spec, tile_spec, tile_spec)
    return jax.shard_map(per_device, mesh=mesh, in_specs=in_specs, out_specs=out_specs, check_vma=False)
```

time: 764 us -> 290 us (0.38)
  waiting for transfers between devices: 470 us -> 0 us
  Pallas kernels: 0 us -> 239 us
  local copies, waits for them, and re-layouts: 140 us -> 0.01 us
  other arithmetic: 84.2 us -> 33.5 us
  matrix products: 45.5 us -> 14.7 us
  between operations: 16 us -> 2.06 us
    reduce_scatter x1 -> x0, waiting for transfers between devices: 357 us -> none  [per_device(): lax.psum_scatter(local_grad, 'dp', scatter_dimension=0, tiled=True) / n_dev]
    pallas_call x0 -> x2, Pallas kernels: none -> 239 us  [the longest x1 163 us: reduce_gradients(): pl.pallas_call(reduce_kernel, out_shape=jax.ShapeDtypeStruct((512, 512),...]
    all_gather x1 -> x0, waiting for transfers between devices: 113 us -> none  [per_device(): lax.all_gather(new_mom.astype(jnp.bfloat16), 'dp', axis=0, tiled=True)]
    convert_element_type x2 -> x0, local copies, waits for them, and re-layouts: 44.3 us -> none  [the longest x1 29.1 us: apply_update(): dir_fc2.astype(jnp.float32) + WEIGHT_DECAY * w_fc2]
    transpose x2 -> x0, local copies, waits for them, and re-layouts: 34.9 us -> none  [grad_blocks(): jnp.einsum('tri,tcj->rcij', x_pad, dy_pad, preferred_element_type=jnp.flo...]
    unnamed x20 -> x6, local copies, waits for them, and re-layouts: 34.2 us -> 0.01 us
    dot_general x6 -> x4, matrix products: 45.5 us -> 14.7 us  [mm(): jnp.dot(a, b, precision=lax.Precision.HIGHEST, preferred_element_type=jnp...]
    convert_element_type x3 -> x0, other arithmetic: 26.3 us -> none  [the longest x1 11.8 us: apply_update(): dir_fc1.astype(jnp.float32) + WEIGHT_DECAY * w_fc1]
  transfers between devices with their start and end apart: 2 -> 0, of which waited for: 2 -> 0; matrix products, arithmetic and copies ran while one was open for 1% -> 0% of each run, Pallas kernels for 0% -> 0%
where the time goes in v1:
time: 290 us; the launch traced here: 289 us
  Pallas kernels  239 us (82%)
  other arithmetic  33.5 us (12%)
  matrix products  14.7 us (5%)
    pallas_call x1, Pallas kernels, reduce_gradients(): pl.pallas_call(reduce_kernel, out_shape=jax.ShapeDtypeStruct((512, 512),...  163 us
    pallas_call x1, Pallas kernels, gather_directions(): pl.pallas_call(gather_kernel, out_shape=(jax.ShapeDtypeStruct((1024, 4096...  76.2 us
    dot_general x4, matrix products, mm(): jnp.dot(a, b, precision=lax.Precision.HIGHEST, preferred_element_type=jnp...  14.7 us
    sub x1, other arithmetic, per_device(): w_fc2 - LEARN_RATE * (dir2.astype(jnp.float32) + WEIGHT_DECAY * w_fc2)  14.6 us
    sub x1, other arithmetic, per_device(): w_fc1 - LEARN_RATE * (dir1.astype(jnp.float32) + WEIGHT_DECAY * w_fc1)  12.8 us

profile of v1, /device:TPU:0, one launch (start us, length us, event | category | flops | bytes accessed | tf_op | source)
XLA Modules:
  0.0 289.3 jit_solution(7308128940986529602)
XLA Ops:
  0.6 162.8 %reduce.1 = f32[512,512]{1,0:T(8,128)} custom-call(bf16[1024,1024]{1,0:T(8,128)(2,1)} %x_in.1, bf16[1024,4096]{1,0:T(8,128)(2,1)} %dy_mid.1, bf16[1024,4096]{1,0:T(8,128)(2,1)} %x_mid.1, bf16[1024,1024]{1,0:T(8,128)(2,1)} %dy_out.1), custom_call_target="tpu_custom_call" | custom-call | tf_op jit(solution)/shard_map/reduce/pallas_call | solution.py:238
  163.4 5.0 %fusion.7 = f32[512,512]{1,0:T(8,128)S(1)} fusion(f32[512,512]{1,0:T(8,128)} %reduce.1, f32[1,512,512]{2,1,0:T(8,128)} %param.20), kind=kOutput, calls=%fused_computation.12 | convolution fusion | flops 1610612736 | bytes 3145728 | tf_op jit(solution)/shard_map/dot_general | solution.py:371
  168.5 3.8 %multiply_reduce_fusion = (f32[]{:T(128)}, f32[512,512]{1,0:T(8,128)S(1)}) fusion(f32[512,512]{1,0:T(8,128)S(1)} %fusion.7, f32[1,512,512]{2,1,0:T(8,128)} %param.21), kind=kOutput, calls=%fused_computation.15 | convolution fusion | flops 1611137024 | bytes 3145732 | tf_op jit(solution)/shard_map/dot_general | solution.py:371
  173.0 3.7 %fusion.9 = (f32[1,512,512]{2,1,0:T(8,128)}, f32[]{:T(128)}) fusion(f32[512,512]{1,0:T(8,128)} %reduce.1, f32[1,512,512]{2,1,0:T(8,128)} %param.22), kind=kLoop, calls=%fused_computation.17 | loop fusion | flops 2359295 | bytes 3145732 | tf_op jit(solution)/shard_map/broadcast_in_dim | solution.py:388
  177.3 2.5 fusion.10
  179.8 76.2 %gather.1 = (bf16[1024,4096]{1,0:T(8,128)(2,1)S(1)}, bf16[4096,1024]{1,0:T(8,128)(2,1)}) custom-call(bf16[512,512]{1,0:T(8,128)(2,1)S(1)} %get-tuple-element.11.dir_ref), custom_call_target="tpu_custom_call" | custom-call | tf_op jit(solution)/shard_map/gather/pallas_call | solution.py:359
  256.1 14.6 %multiply_subtract_fusion = f32[4096,1024]{1,0:T(8,128)} fusion(f32[4096,1024]{1,0:T(8,128)} %param.17, bf16[4096,1024]{1,0:T(8,128)(2,1)} %get-tuple-element.9), kind=kLoop, calls=%fused_computation | loop fusion | flops 20971520 | bytes 41943040 | tf_op jit(solution)/shard_map/sub | solution.py:387
  270.6 0.0 copy-start
  270.6 0.0 copy-start.1
  270.6 0.0 copy-start.2
  270.6 12.8 %multiply_subtract_fusion.1 = f32[1024,4096]{1,0:T(8,128)} fusion(f32[1024,4096]{1,0:T(8,128)} %param.16, bf16[1024,4096]{1,0:T(8,128)(2,1)S(1)} %get-tuple-element.8), kind=kLoop, calls=%fused_computation.1 | loop fusion | flops 20971520 | bytes 41943040 | tf_op jit(solution)/shard_map/sub | solution.py:386
  283.4 0.0 copy-done
  283.4 0.0 copy-done.1
  283.4 3.0 %fusion.1 = f32[1,512,512]{2,1,0:T(8,128)} fusion(f32[512,512]{1,0:T(8,128)S(1)} %copy-done, f32[1,512,512]{2,1,0:T(8,128)S(1)} %copy-done.1), kind=kOutput, calls=%fused_computation.5 | convolution fusion | flops 1611399168 | bytes 3145728 | tf_op jit(solution)/shard_map/dot_general | solution.py:371
  286.4 0.0 copy-done.2
  286.4 2.9 %fusion.3 = f32[1,512,512]{2,1,0:T(8,128)} fusion(f32[512,512]{1,0:T(8,128)S(1)} %copy-done, f32[1,512,512]{2,1,0:T(8,128)S(1)} %copy-done.2), kind=kOutput, calls=%fused_computation.8 | convolution fusion | flops 1611399168 | bytes 3145728 | tf_op jit(solution)/shard_map/dot_general | solution.py:371
Async XLA Ops:
  270.6 12.8 %copy-start = (f32[512,512]{1,0:T(8,128)S(1)}, f32[512,512]{1,0:T(8,128)}, u32[]{:S(2)}) copy-start(f32[512,512]{1,0:T(8,128)} %reduce.1) | copy-start | bytes 3145732
  270.6 12.8 %copy-start.1 = (f32[1,512,512]{2,1,0:T(8,128)S(1)}, f32[1,512,512]{2,1,0:T(8,128)}, u32[]{:S(2)}) copy-start(f32[1,512,512]{2,1,0:T(8,128)} %param.19) | copy-start | bytes 3145732
  270.6 15.8 %copy-start.2 = (f32[1,512,512]{2,1,0:T(8,128)S(1)}, f32[1,512,512]{2,1,0:T(8,128)}, u32[]{:S(2)}) copy-start(f32[1,512,512]{2,1,0:T(8,128)} %param.18) | copy-start | bytes 3145732

commit v2 on v1

--- a/solution.py
+++ b/solution.py
@@ -29,13 +29,15 @@
     return me // 8, (me // 4) % 2, (me // 2) % 2, me % 2
 
 
-def greet(z, y, x, c):
-    barrier = pltpu.get_barrier_semaphore()
+def greet_signal(z, y, x, c):
     peers = [dev(z, y, 1 - x, c), dev(z, 1 - y, x, c), dev(z, y, x, 1 - c)]
     peers += [dev((z + k) % 4, y, x, c) for k in (1, 2, 3)]
     for peer in peers:
-        pl.semaphore_signal(barrier, inc=1, device_id=peer, device_id_type=MESH)
-    pl.semaphore_wait(barrier, len(peers))
+        pl.semaphore_signal(pltpu.get_barrier_semaphore(), inc=1, device_id=peer, device_id_type=MESH)
+
+
+def greet_wait():
+    pl.semaphore_wait(pltpu.get_barrier_semaphore(), 6)
 
 
 def remote(src, dst, send_sem, recv_sem, peer):
@@ -78,7 +80,8 @@
         here(kind, i).wait()
         there(kind, i).wait_recv()
 
-    greet(z, y, x, c)
+    greet_signal(z, y, x, c)
+    greet_wait()
 
     zb = [(z + h) % 4 for h in HOPS]
     first1 = [zb[0] < 2, (zb[1] < 2) & (zb[0] >= 2)]
@@ -250,38 +253,73 @@
     )(x_in, dy_mid, x_mid, dy_out)
 
 
-def gather_kernel(dir_ref, d1, d2, buf, isem, zs, zr, xs, xr, ys, yr, xds, xdr, yds, ydr, cs, cr, osem):
+def gather_kernel(grad_in, rl_in, rr_in, sq_in, mom_in, sl_in, sr_in, w1_in, w2_in, new_left, new_right, new_sq, new_mom, w,
+                  buf, grad, rl, rr, pre, isem, zs, zr, xs, xr, ys, yr, xds, xdr, yds, ydr, cs, cr):
     z, y, x, c = coords()
     xp, yp, cp = dev(z, y, 1 - x, c), dev(z, 1 - y, x, c), dev(z, y, x, 1 - c)
 
     def blk(zb, yb, xb, cb):
         return dev(zb, yb, xb, cb)[0]
 
-    bring = pltpu.make_async_copy(dir_ref, buf.at[blk(z, y, x, c)], isem)
-    bring.start()
-    greet(z, y, x, c)
-    bring.wait()
+    pairs = [(grad_in, grad), (rl_in, rl), (rr_in, rr), (sq_in, new_sq), (mom_in, new_mom), (sl_in, new_left), (sr_in, new_right), (w2_in, w.at[pl.ds(4096, 4096)])]
+    pairs += [(w1_in.at[:, pl.ds(1024 * n, 1024)], w.at[pl.ds(1024 * n, 1024)]) for n in range(4)]
+    loads = [pltpu.make_async_copy(src, dst, isem.at[i]) for i, (src, dst) in enumerate(pairs)]
+    for load in loads[:5]:
+        load.start()
+    greet_signal(z, y, x, c)
+
+    b0 = blk(z, y, x, c)
+    for load in loads[:4]:
+        load.wait()
+    for load in loads[5:]:
+        load.start()
+    pre[...] = mm(rl[...], grad[...])
+    rl[...] = mm(pre[...], rr[...])
+
+    def strip_of(i):
+        return pl.ds(pl.multiple_of(i * 64, 64), 64)
+
+    def norms(i, sums):
+        r = strip_of(i)
+        g, p = grad[r], rl[r]
+        sq = STAT_DECAY * new_sq[r] + (1.0 - STAT_DECAY) * g * g
+        new_sq[r] = sq
+        h = g / (jnp.sqrt(sq / BIAS_CORR) + GRAFT_EPS)
+        return sums[0] + jnp.sum(h * h), sums[1] + jnp.sum(p * p)
+
+    graft_sum, pre_sum = lax.fori_loop(0, 8, norms, (jnp.float32(0.0), jnp.float32(0.0)))
+    loads[4].wait()
+    ones = jnp.ones((64, 512), jnp.float32)
+    scale = jnp.sqrt(graft_sum * ones) / jnp.sqrt(pre_sum * ones)
+
+    def momentum_step(i, _):
+        r = strip_of(i)
+        mom = MOM_DECAY * new_mom[r] + rl[r] * scale
+        new_mom[r] = mom
+        buf[b0, r] = mom.astype(jnp.bfloat16)
+        return 0
+
+    lax.fori_loop(0, 8, momentum_step, 0)
+    greet_wait()
 
     zb = [(z + 4 - h) % 4 for h in GATHER_HOPS]
     spots = [(y, x), (1 - y, x), (y, 1 - x), (1 - y, 1 - x)]
 
-    def put(b, zk, n):
-        def one():
-            return pltpu.make_async_copy(buf.at[b], d1.at[pl.ds(pl.multiple_of((b // 8) * 512, 512), 512), pl.ds(pl.multiple_of((b % 8) * 512, 512), 512)], osem.at[n])
-
-        def two():
-            return pltpu.make_async_copy(buf.at[b], d2.at[pl.ds(pl.multiple_of(((b - 16) // 2) * 512, 512), 512), pl.ds(pl.multiple_of((b % 2) * 512, 512), 512)], osem.at[n])
-
-        @pl.when(zk < 2)
-        def _():
-            one().start()
-
-        @pl.when(zk >= 2)
-        def _():
-            two().start()
-
-    def whole(ref, b):
-        return ref.at[b]
+    def step(w, b, row, col):
+        def strip(i, _):
+            r = pl.ds(pl.multiple_of(row * 512 + i * 64, 64), 64)
+            cc = pl.ds(pl.multiple_of(col * 512, 512), 512)
+            old = w[r, cc]
+            d = buf[b, pl.ds(pl.multiple_of(i * 64, 64), 64), :].astype(jnp.float32)
+            w[r, cc] = old - LEARN_RATE * (d + WEIGHT_DECAY * old)
+            return 0
+
+        lax.fori_loop(0, 8, strip, 0)
+
+    def apply(b, zk):
+        first = zk < 2
+        col = jnp.where(first, b % 8, b % 2)
+        step(w, b, jnp.where(first, (col // 2) * 2 + b // 8, 8 + (b - 16) // 2), col % 2)
 
     def part(ref, b, h):
         return ref.at[b, pl.ds(h * 256, 256)]
@@ -304,41 +342,51 @@
     def zcopy(k, b, peer):
         return remote(buf.at[b], buf.at[b], zs.at[k - 1], zr.at[k - 1], peer)
 
-    def open_group(k):
-        b = blk(zb[k], y, x, c)
-        xcopy(k, b).start()
-        ycopy(k, b).start()
-        ccopy(k, 0, b).start()
-        put(b, zb[k], k * 8)
-
-    b0 = blk(z, y, x, c)
     xcopy(0, b0).start()
     ycopy(0, b0).start()
     for k in (1, 2, 3):
         zcopy(k, b0, dev((z + GATHER_HOPS[k]) % 4, y, x, c)).start()
     ccopy(0, 0, b0).start()
-    put(b0, z, 0)
+    for load in loads[5:7]:
+        load.wait()
+    pre[...] = mm(grad[...], grad[...], ((1,), (1,)))
+    rr[...] = mm(grad[...], grad[...], ((0,), (0,)))
+
+    def stats(i, _):
+        r = strip_of(i)
+        new_left[r] = STAT_DECAY * new_left[r] + (1.0 - STAT_DECAY) * pre[r]
+        new_right[r] = STAT_DECAY * new_right[r] + (1.0 - STAT_DECAY) * rr[r]
+        return 0
+
+    lax.fori_loop(0, 8, stats, 0)
+    for load in loads[7:]:
+        load.wait()
     for k in range(4):
-        by, bx, bd = [blk(zb[k], yy, xx, c) for yy, xx in spots[1:]]
+        b, by, bx, bd = [blk(zb[k], yy, xx, c) for yy, xx in spots]
+        others = [blk(zb[k], yy, xx, 1 - c) for yy, xx in spots]
         ycopy(k, by).wait_recv()
         xdiag(k, by).start()
         ccopy(k, 1, by).start()
-        put(by, zb[k], k * 8 + 1)
         xcopy(k, bx).wait_recv()
         ydiag(k, bx).start()
         ccopy(k, 2, bx).start()
-        put(bx, zb[k], k * 8 + 2)
         if k < 3:
-            zcopy(k + 1, blk(zb[k + 1], y, x, c), xp).wait_recv()
-            open_group(k + 1)
+            nb = blk(zb[k + 1], y, x, c)
+            zcopy(k + 1, nb, xp).wait_recv()
+            xcopy(k + 1, nb).start()
+            ycopy(k + 1, nb).start()
+            ccopy(k + 1, 0, nb).start()
+        for t in (b, by, bx):
+            apply(t, zb[k])
+        for i in range(3):
+            ccopy(k, i, others[i]).wait_recv()
+            apply(others[i], zb[k])
         xdiag(k, bd).wait_recv()
         ydiag(k, bd).wait_recv()
         ccopy(k, 3, bd).start()
-        put(bd, zb[k], k * 8 + 3)
-        for i, (yy, xx) in enumerate(spots):
-            bo = blk(zb[k], yy, xx, 1 - c)
-            ccopy(k, i, bo).wait_recv()
-            put(bo, zb[k], k * 8 + 4 + i)
+        apply(bd, zb[k])
+        ccopy(k, 3, others[3]).wait_recv()
+        apply(others[3], zb[k])
     for k in range(4):
         xcopy(k, b0).wait_send()
         ycopy(k, b0).wait_send()
@@ -348,43 +396,59 @@
             ccopy(k, i, b0).wait_send()
         if k:
             zcopy(k, b0, xp).wait_send()
-    for n in range(32):
-        pltpu.make_async_copy(buf.at[0], d1.at[pl.ds(0, 512), pl.ds(0, 512)], osem.at[n]).wait()
-
-
-def gather_directions(own_dir):
-    bf = jnp.bfloat16
+
+
+def finish_step(grad, root_left, root_right, graft_sq, momentum, stat_left, stat_right, w_fc1, w_fc2):
+    bf, f32 = jnp.bfloat16, jnp.float32
     dma = pltpu.SemaphoreType.DMA
     any_spec = pl.BlockSpec(memory_space=pl.ANY)
+    vmem_spec = pl.BlockSpec(memory_space=pltpu.VMEM)
+    tile = pltpu.VMEM((512, 512), f32)
     return pl.pallas_call(
         gather_kernel,
-        out_shape=(jax.ShapeDtypeStruct((1024, 4096), bf), jax.ShapeDtypeStruct((4096, 1024), bf)),
-        in_specs=[any_spec],
-        out_specs=(any_spec, any_spec),
-        scratch_shapes=[pltpu.VMEM((32, 512, 512), bf), dma, dma((3,)), dma((3,))] + [dma((4,))] * 8 + [dma((4, 4)), dma((4, 4)), dma((32,))],
-        compiler_params=pltpu.CompilerParams(collective_id=1, has_side_effects=True, vmem_limit_bytes=40 * 2 ** 20),
+        out_shape=(tile, tile, tile, tile, pltpu.VMEM((8192, 1024), f32)),
+        in_specs=[any_spec] * 9,
+        out_specs=(vmem_spec,) * 5,
+        scratch_shapes=[pltpu.VMEM((32, 512, 512), bf)] + [pltpu.VMEM((512, 512), f32)] * 4 + [dma((12,)), dma((3,)), dma((3,))] + [dma((4,))] * 8 + [dma((4, 4)), dma((4, 4))],
+        compiler_params=pltpu.CompilerParams(collective_id=1, has_side_effects=True, vmem_limit_bytes=26 * 2 ** 20),
         name="gather",
-    )(own_dir)
-
-
-def mm(a, b):
-    return jnp.dot(a, b, precision=lax.Precision.HIGHEST, preferred_element_type=jnp.float32)
+    )(grad, root_left, root_right, graft_sq, momentum, stat_left, stat_right, w_fc1, w_fc2)
+
+
+def flush_kernel(left, right, sq, mom, w, left_out, right_out, sq_out, mom_out, w1_out, w2_out, sem):
+    pairs = [(w.at[pl.ds(1024 * n, 1024)], w1_out.at[:, pl.ds(1024 * n, 1024)]) for n in range(4)]
+    pairs += [(w.at[pl.ds(4096, 4096)], w2_out), (left, left_out), (right, right_out), (sq, sq_out), (mom, mom_out)]
+    out = [pltpu.make_async_copy(src, dst, sem.at[i]) for i, (src, dst) in enumerate(pairs)]
+    for o in out:
+        o.start()
+    for o in out:
+        o.wait()
+
+
+def flush(left, right, sq, mom, w, shape1, shape2):
+    any_spec = pl.BlockSpec(memory_space=pl.ANY)
+    tile = jax.ShapeDtypeStruct(left.shape, left.dtype)
+    values = [pltpu.with_memory_space_constraint(v, pltpu.VMEM) for v in (left, right, sq, mom, w)]
+    return pl.pallas_call(
+        flush_kernel,
+        out_shape=(tile, tile, tile, tile, jax.ShapeDtypeStruct(shape1, w.dtype), jax.ShapeDtypeStruct(shape2, w.dtype)),
+        in_specs=[pl.BlockSpec(memory_space=pltpu.VMEM)] * 5,
+        out_specs=(any_spec,) * 6,
+        scratch_shapes=[pltpu.SemaphoreType.DMA((9,))],
+        compiler_params=pltpu.CompilerParams(vmem_limit_bytes=2 ** 20),
+        name="flush",
+    )(*values)
+
+
+def mm(a, b, dims=((1,), (0,))):
+    return lax.dot_general(a, b, (dims, ((), ())), precision=lax.Precision.HIGHEST, preferred_element_type=jnp.float32)
 
 
 def solution(mesh):
     def per_device(x_in, dy_mid, x_mid, dy_out, w_fc1, w_fc2, stat_left, stat_right, root_left, root_right, graft_sq, momentum):
         grad = reduce_gradients(x_in, dy_mid, x_mid, dy_out)
-        precond = mm(mm(root_left[0], grad), root_right[0])
-        new_sq = STAT_DECAY * graft_sq[0] + (1.0 - STAT_DECAY) * grad * grad
-        graft_dir = grad / (jnp.sqrt(new_sq / BIAS_CORR) + GRAFT_EPS)
-        graft_norm = jnp.sqrt(jnp.sum(graft_dir * graft_dir))
-        pre_norm = jnp.sqrt(jnp.sum(precond * precond))
-        new_mom = MOM_DECAY * momentum[0] + precond * (graft_norm / pre_norm)
-        dir1, dir2 = gather_directions(new_mom.astype(jnp.bfloat16))
-        new_left = STAT_DECAY * stat_left[0] + (1.0 - STAT_DECAY) * mm(grad, grad.T)
-        new_right = STAT_DECAY * stat_right[0] + (1.0 - STAT_DECAY) * mm(grad.T, grad)
-        new_w1 = w_fc1 - LEARN_RATE * (dir1.astype(jnp.float32) + WEIGHT_DECAY * w_fc1)
-        new_w2 = w_fc2 - LEARN_RATE * (dir2.astype(jnp.float32) + WEIGHT_DECAY * w_fc2)
+        done = finish_step(grad, root_left[0], root_right[0], graft_sq[0], momentum[0], stat_left[0], stat_right[0], w_fc1, w_fc2)
+        new_left, new_right, new_sq, new_mom, new_w1, new_w2 = flush(*done, w_fc1.shape, w_fc2.shape)
         return new_w1, new_w2, new_left[None], new_right[None], new_sq[None], new_mom[None]
 
     row_spec = P('dp', None)

time: 290 us -> 258 us (0.89)
  other arithmetic: 33.5 us -> 0 us
  Pallas kernels: 239 us -> 257 us
  matrix products: 14.7 us -> 0 us
    sub x2 -> x0, other arithmetic: 27.4 us -> none  [the longest x1 14.6 us: per_device(): w_fc2 - LEARN_RATE * (dir2.astype(jnp.float32) + WEIGHT_DECAY * w_fc2)]
    pallas_call x1 -> x2, Pallas kernels: 76.2 us -> 94.4 us  [the longest x1 82.2 us: finish_step(): pl.pallas_call(gather_kernel, out_shape=(tile, tile, tile, tile, pltpu.VM...]
    dot_general x4 -> x0, matrix products: 14.7 us -> none  [mm(): jnp.dot(a, b, precision=lax.Precision.HIGHEST, preferred_element_type=jnp...]
    broadcast_in_dim x2 -> x0, other arithmetic: 6.13 us -> none  [the longest x1 3.68 us: per_device(): new_sq[None]]
where the time goes in v2:
time: 258 us
  Pallas kernels  257 us (100%)
    pallas_call x1, Pallas kernels, reduce_gradients(): pl.pallas_call(reduce_kernel, out_shape=jax.ShapeDtypeStruct((512, 512),...  163 us
    pallas_call x1, Pallas kernels, finish_step(): pl.pallas_call(gather_kernel, out_shape=(tile, tile, tile, tile, pltpu.VM...  82.2 us
    pallas_call x1, Pallas kernels, flush(): pl.pallas_call(flush_kernel, out_shape=(tile, tile, tile, tile, jax.Shape...  12.2 us

profile of v2, /device:TPU:0, one launch (start us, length us, event | category | flops | bytes accessed | tf_op | source)
XLA Modules:
  0.0 257.8 jit_solution(11016322368653588440)
XLA Ops:
  0.6 162.7 %reduce.1.grad_in = f32[512,512]{1,0:T(8,128)} custom-call(bf16[1024,1024]{1,0:T(8,128)(2,1)} %x_in.1, bf16[1024,4096]{1,0:T(8,128)(2,1)} %dy_mid.1, bf16[1024,4096]{1,0:T(8,128)(2,1)} %x_mid.1, bf16[1024,1024]{1,0:T(8,128)(2,1)} %dy_out.1), custom_call_target="tpu_custom_call" | custom-call | tf_op jit(solution)/shard_map/reduce/pallas_call | solution.py:241
  163.4 82.2 %gather.1 = (f32[512,512]{1,0:T(8,128)S(1)}, f32[512,512]{1,0:T(8,128)S(1)}, f32[512,512]{1,0:T(8,128)S(1)}, f32[512,512]{1,0:T(8,128)S(1)}, f32[8192,1024]{1,0:T(8,128)S(1)}) custom-call(f32[512,512]{1,0:T(8,128)} %reduce.1.grad_in, f32[512,512]{1,0:T(8,128)} %bitcast.10, f32[512,512]{1,0:T(8,128)} %bitcast.11, f32[512,512]{1,0:T(8,128)} %bitcast.12, ...), custom_call_target="tpu_custom_call" | custom-call | tf_op jit(solution)/shard_map/gather/pallas_call | solution.py:407
  245.6 12.2 %flush.1 = (f32[512,512]{1,0:T(8,128)}, f32[512,512]{1,0:T(8,128)}, f32[512,512]{1,0:T(8,128)}, f32[512,512]{1,0:T(8,128)}, f32[1024,4096]{1,0:T(8,128)}, /*index=5*/f32[4096,1024]{1,0:T(8,128)}) custom-call(f32[512,512]{1,0:T(8,128)S(1)} %get-tuple-element.17.left, f32[512,512]{1,0:T(8,128)S(1)} %get-tuple-element.18.right, ...), custom_call_target="tpu_custom_call" | custom-call | tf_op jit(solution)/shard_map/flush/pallas_call | solution.py:432

commit v3 on v2

--- a/solution.py
+++ b/solution.py
@@ -16,7 +16,9 @@
 BIAS_CORR = 1.0 - STAT_DECAY ** STEP
 
 MESH = pl.DeviceIdType.MESH
-HOPS = (2, 3, 1, 0)
+HOPS = (3, 2, 1, 0)
+PLANE = 208
+LINE = 512 - 2 * PLANE
 GATHER_HOPS = (0, 1, 3, 2)
 
 
@@ -44,7 +46,7 @@
     return pltpu.make_async_remote_copy(src_ref=src, dst_ref=dst, send_sem=send_sem, recv_sem=recv_sem, device_id=peer, device_id_type=MESH)
 
 
-def reduce_kernel(x_in, dy_mid, x_mid, dy_out, out_ref, xi, dm, xm, do, acc, rx, ry, rz, lsem, psem, qsem, xs, xr, ys, yr, zs, zr, osem):
+def reduce_kernel(x_in, dy_mid, x_mid, dy_out, out_ref, xi, dm, xm, do, acc, rx, ry, rx3, ry3, rz, ro, ri, lsem, psem, qsem, xs, xr, ys, yr, zs, zr, ls, lr, ms, mr, osem):
     z, y, x, c = coords()
     rows = x_in.shape[0]
     bd = 512
@@ -83,7 +85,13 @@
     greet_signal(z, y, x, c)
     greet_wait()
 
-    zb = [(z + h) % 4 for h in HOPS]
+    low = z < 2
+    end = (z == 0) | (z == 3)
+    hop = [jnp.where(low, h, (4 - h) % 4) for h in HOPS]
+    zb = [(z + h) % 4 for h in hop]
+    inner = dev(jnp.where(low, z + 1, z - 1), y, x, c)
+    outer = dev(jnp.where(low, 0, 3), y, x, c)
+    far = dev(jnp.where(low, 3, 0), y, x, c)
     first1 = [zb[0] < 2, (zb[1] < 2) & (zb[0] >= 2)]
     first2 = [zb[0] >= 2, (zb[1] >= 2) & (zb[0] < 2)]
     first1 += [(zb[2] < 2) & (zb[0] >= 2) & (zb[1] >= 2), zb[0] < 0]
@@ -110,16 +118,50 @@
 
     def dots(lhs, rhs, dst):
         for h in range(2):
-            dst[h] = lax.dot_general(lhs[:, h * half:(h + 1) * half], rhs[...], (((0,), (0,)), ((), ())), preferred_element_type=jnp.float32)
-
-    def send_one(k, q, j):
+            dst[h * half:(h + 1) * half] = lax.dot_general(lhs[:, h * half:(h + 1) * half], rhs[...], (((0,), (0,)), ((), ())), preferred_element_type=jnp.float32)
+
+    def size(k):
+        return half if k == 3 else PLANE
+
+    def rows_of(k, h):
+        return pl.ds(h * size(k), size(k))
+
+    def slot_x(k, i):
+        return rx3.at[i] if k == 3 else rx.at[k, i]
+
+    def slot_y(k, i):
+        return ry3.at[i] if k == 3 else ry.at[k, i]
+
+    def send_x(k, i, j, h):
+        return remote(acc.at[k, j, rows_of(k, h)], slot_x(k, i), xs.at[k, i], xr.at[k, i], xp)
+
+    def send_y(k, i, j, h):
+        return remote(acc.at[k, j, rows_of(k, h)], slot_y(k, i), ys.at[k, i], yr.at[k, i], yp)
+
+    def send_one(q, j):
         @pl.when(q < 2)
         def _():
-            remote(acc.at[k, j, 0], rx.at[k, q], xs.at[k, q], xr.at[k, q], xp).start()
+            remote(acc.at[0, j, rows_of(0, 0)], rx.at[0, q], xs.at[0, q], xr.at[0, q], xp).start()
 
         @pl.when(q % 2 == 0)
         def _():
-            remote(acc.at[k, j, 1], ry.at[k, q // 2], ys.at[k, q // 2], yr.at[k, q // 2], yp).start()
+            remote(acc.at[0, j, rows_of(0, 1)], ry.at[0, q // 2], ys.at[0, q // 2], yr.at[0, q // 2], yp).start()
+
+    line = pl.ds(2 * PLANE, LINE)
+
+    def inward(k, n, q):
+        return remote(acc.at[k, order_of(q), line], ro.at[n, q], ls.at[n, q], lr.at[n, q], inner)
+
+    def across(k, n, q, peer):
+        return remote(acc.at[k, order_of(q), line], ri.at[n, q], ms.at[n, q], mr.at[n, q], peer)
+
+    def order_of(q):
+        return order[q] if isinstance(q, int) else pick(order, q)
+
+    def pass_on(n, q):
+        inward(0, n, q).wait_recv()
+        acc[n + 1, order_of(q), line] += ro[n, q]
+        across(n + 1, n, q, inner).start()
 
     def pick(values, i):
         out = values[-1]
@@ -156,67 +198,134 @@
                 arrive("xm", t)
                 dots(xm.at[t], do, acc.at[k, j])
 
-            @pl.when(k < 2)
-            def _():
-                send_one(k, q, j)
+            @pl.when(k < 1)
+            def _():
+                send_one(q, j)
+
+            @pl.when(end & (k < 3))
+            def _():
+                inward(k, k, q).start()
+
+            @pl.when(jnp.logical_not(end) & (k == 2))
+            def _():
+                pass_on(0, q)
 
             return 0
 
         return lax.fori_loop(0, 4, tile, 0)
 
-    lax.fori_loop(0, 4, group, 0)
-
-    def add(k, j, h, ref):
-        acc[k, j, h] += ref[...]
-
-    def got(buf, ss, rs, k, i):
-        remote(buf.at[k, i], buf.at[k, i], ss.at[k, i], rs.at[k, i], xp).wait_recv()
+    lax.fori_loop(0, 2, group, 0)
+
+    def add(k, j, where, ref):
+        acc[k, j, where] += ref[...]
 
     def start_one(k):
-        for q in range(3):
-            if q < 2:
-                remote(acc.at[k, order[q], 0], rx.at[k, q], xs.at[k, q], xr.at[k, q], xp).start()
-            if q % 2 == 0:
-                remote(acc.at[k, order[q], 1], ry.at[k, q // 2], ys.at[k, q // 2], yr.at[k, q // 2], yp).start()
+        send_x(k, 0, order[0], 0).start()
+        send_y(k, 0, order[0], 1).start()
+        send_x(k, 1, order[1], 0).start()
+        send_y(k, 1, order[2], 1).start()
 
     def start_two(k):
-        got(rx, xs, xr, k, 0)
-        add(k, order[2], 0, rx.at[k, 0])
-        remote(acc.at[k, order[2], 0], ry.at[k, 2], ys.at[k, 2], yr.at[k, 2], yp).start()
-        got(ry, ys, yr, k, 0)
-        add(k, order[1], 1, ry.at[k, 0])
-        remote(acc.at[k, order[1], 1], rx.at[k, 2], xs.at[k, 2], xr.at[k, 2], xp).start()
+        send_x(k, 0, own, 0).wait_recv()
+        add(k, order[2], rows_of(k, 0), slot_x(k, 0))
+        send_y(k, 2, order[2], 0).start()
+        send_y(k, 0, own, 1).wait_recv()
+        add(k, order[1], rows_of(k, 1), slot_y(k, 0))
+        send_x(k, 2, order[1], 1).start()
+
+    def send_z(k, h):
+        n = jnp.where(end, k, (0, 1, 3)[k])
+        peer = (jnp.where(end, inner[0], (outer, far, inner)[k][0]),)
+        return remote(acc.at[k, own, rows_of(k, h)], rz.at[n, h], zs.at[k, h], zr.at[n, h], peer)
+
+    def got_z(n, h):
+        remote(rz.at[n, h], rz.at[n, h], zs.at[0, h], zr.at[n, h], inner).wait_recv()
+
+    def relay(k):
+        @pl.when(jnp.logical_not(end))
+        def _():
+            for h in range(2):
+                got_z(k - 1, h)
+                add(k, own, rows_of(k, h), rz.at[k - 1, h])
+                send_z(k, h).start()
+
+    def leave(k, h):
+        if k == 0:
+            send_z(k, h).start()
+        elif k < 3:
+            @pl.when(end)
+            def _():
+                send_z(k, h).start()
 
     def finish_plane(k):
-        got(rx, xs, xr, k, 1)
-        add(k, own, 0, rx.at[k, 1])
-        got(ry, ys, yr, k, 1)
-        add(k, own, 1, ry.at[k, 1])
-        for h, (buf, ss, rs) in enumerate(((ry, ys, yr), (rx, xs, xr))):
-            got(buf, ss, rs, k, 2)
-            add(k, own, h, buf.at[k, 2])
-            if k < 3:
-                remote(acc.at[k, own, h], rz.at[k, h], zs.at[k, h], zr.at[k, h], dev(zb[k], y, x, c)).start()
+        send_x(k, 1, own, 0).wait_recv()
+        add(k, own, rows_of(k, 0), slot_x(k, 1))
+        send_y(k, 1, own, 1).wait_recv()
+        add(k, own, rows_of(k, 1), slot_y(k, 1))
+        send_y(k, 2, own, 0).wait_recv()
+        add(k, own, rows_of(k, 0), slot_y(k, 2))
+        leave(k, 0)
+        send_x(k, 2, own, 1).wait_recv()
+        add(k, own, rows_of(k, 1), slot_x(k, 2))
+        leave(k, 1)
+
+    def line_first(n):
+        @pl.when(jnp.logical_not(end))
+        def _():
+            for q in range(4):
+                pass_on(n, q)
+
+    def line_second():
+        @pl.when(jnp.logical_not(end))
+        def _():
+            for q in range(4):
+                across(0, 0, q, inner).wait_recv()
+                add(0, order[q], line, ri.at[0, q])
+                remote(acc.at[0, order[q], line], ri.at[0, q], ms.at[2, q], mr.at[0, q], outer).start()
+
+    def line_last():
+        @pl.when(end)
+        def _():
+            for q in range(4):
+                across(0, 0, q, inner).wait_recv()
+                add(3, order[q], line, ri.at[0, q])
+
+        @pl.when(jnp.logical_not(end))
+        def _():
+            for q in range(4):
+                inward(0, 2, q).wait_recv()
+                add(3, order[q], line, ro.at[2, q])
+                across(0, 1, q, inner).wait_recv()
+                add(3, order[q], line, ri.at[1, q])
 
     start_two(0)
+    start_one(1)
+    lax.fori_loop(2, 4, group, 0)
+    finish_plane(0)
+    start_two(1)
     start_one(2)
-    start_two(1)
-    finish_plane(0)
+    line_first(1)
+    line_second()
+    finish_plane(1)
     start_two(2)
+    line_last()
     start_one(3)
-    finish_plane(1)
+    relay(1)
     finish_plane(2)
     start_two(3)
+    relay(2)
     finish_plane(3)
 
-    for k in range(3):
+    for n in range(2):
         for h in range(2):
-            remote(rz.at[k, h], rz.at[k, h], zs.at[k, h], zr.at[k, h], xp).wait_recv()
-            add(3, own, h, rz.at[k, h])
+            slot = jnp.where(end, n, n + 2)
+            got_z(slot, h)
+            add(3, own, rows_of(0, h), rz.at[slot, h])
     outs = []
     for h in range(2):
-        acc[3, own, h] = acc[3, own, h] * (1.0 / 32.0)
-        o = pltpu.make_async_copy(acc.at[3, own, h], out_ref.at[pl.ds(h * half, half)], osem.at[h])
+        part = pl.ds(h * half, half)
+        acc[3, own, part] = acc[3, own, part] * (1.0 / 32.0)
+        o = pltpu.make_async_copy(acc.at[3, own, part], out_ref.at[part], osem.at[h])
         o.start()
         outs.append(o)
     for s in range(15):
@@ -224,11 +333,25 @@
         there(kind, i).wait_send()
     for k in range(4):
         for i in range(3):
-            remote(rx.at[k, i], rx.at[k, i], xs.at[k, i], xr.at[k, i], xp).wait_send()
-            remote(ry.at[k, i], ry.at[k, i], ys.at[k, i], yr.at[k, i], yp).wait_send()
+            send_x(k, i, own, 0).wait_send()
+            send_y(k, i, own, 0).wait_send()
     for k in range(3):
         for h in range(2):
-            remote(rz.at[k, h], rz.at[k, h], zs.at[k, h], zr.at[k, h], xp).wait_send()
+            send_z(k, h).wait_send()
+
+    @pl.when(end)
+    def _():
+        for n in range(3):
+            for q in range(4):
+                inward(0, n, q).wait_send()
+
+    @pl.when(jnp.logical_not(end))
+    def _():
+        for q in range(4):
+            for n in range(2):
+                across(0, n, q, inner).wait_send()
+            remote(acc.at[0, order[q], line], ri.at[0, q], ms.at[2, q], mr.at[0, q], outer).wait_send()
+
     for o in outs:
         o.wait()
 
@@ -245,8 +368,11 @@
         out_specs=any_spec,
         scratch_shapes=[
             pltpu.VMEM((2, rows, 512), bf), pltpu.VMEM((4, rows, 512), bf), pltpu.VMEM((8, rows, 512), bf), pltpu.VMEM((rows, 512), bf),
-            pltpu.VMEM((4, 4, 2, 256, 512), f32), pltpu.VMEM((4, 3, 256, 512), f32), pltpu.VMEM((4, 3, 256, 512), f32), pltpu.VMEM((3, 2, 256, 512), f32),
-            dma((15,)), dma((15,)), dma((15,)), dma((4, 3)), dma((4, 3)), dma((4, 3)), dma((4, 3)), dma((3, 2)), dma((3, 2)), dma((2,)),
+            pltpu.VMEM((4, 4, 512, 512), f32), pltpu.VMEM((3, 3, PLANE, 512), f32), pltpu.VMEM((3, 3, PLANE, 512), f32),
+            pltpu.VMEM((3, 256, 512), f32), pltpu.VMEM((3, 256, 512), f32), pltpu.VMEM((4, 2, PLANE, 512), f32),
+            pltpu.VMEM((3, 4, LINE, 512), f32), pltpu.VMEM((2, 4, LINE, 512), f32),
+            dma((15,)), dma((15,)), dma((15,)), dma((4, 3)), dma((4, 3)), dma((4, 3)), dma((4, 3)), dma((3, 2)), dma((4, 2)),
+            dma((3, 4)), dma((3, 4)), dma((3, 4)), dma((2, 4)), dma((2,)),
         ],
         compiler_params=pltpu.CompilerParams(collective_id=0, has_side_effects=True, vmem_limit_bytes=67043328),
         name="reduce",

time: 258 us -> 227 us (0.88)
  Pallas kernels: 257 us -> 226 us
    pallas_call x1, Pallas kernels: 163 us -> 131 us  [reduce_gradients(): pl.pallas_call(reduce_kernel, out_shape=jax.ShapeDtypeStruct((512, 512),...]
where the time goes in v3:
time: 227 us
  Pallas kernels  226 us (100%)
    pallas_call x1, Pallas kernels, reduce_gradients(): pl.pallas_call(reduce_kernel, out_shape=jax.ShapeDtypeStruct((512, 512),...  131 us
    pallas_call x1, Pallas kernels, finish_step(): pl.pallas_call(gather_kernel, out_shape=(tile, tile, tile, tile, pltpu.VM...  82.6 us
    pallas_call x1, Pallas kernels, flush(): pl.pallas_call(flush_kernel, out_shape=(tile, tile, tile, tile, jax.Shape...  12.2 us

profile of v3, /device:TPU:0, one launch (start us, length us, event | category | flops | bytes accessed | tf_op | source)
XLA Modules:
  0.0 226.5 jit_solution(1919357667168931587)
XLA Ops:
  0.6 131.0 %reduce.1.grad_in = f32[512,512]{1,0:T(8,128)} custom-call(bf16[1024,1024]{1,0:T(8,128)(2,1)} %x_in.1, bf16[1024,4096]{1,0:T(8,128)(2,1)} %dy_mid.1, bf16[1024,4096]{1,0:T(8,128)(2,1)} %x_mid.1, bf16[1024,1024]{1,0:T(8,128)(2,1)} %dy_out.1), custom_call_target="tpu_custom_call" | custom-call | tf_op jit(solution)/shard_map/reduce/pallas_call | solution.py:364
  131.6 82.6 %gather.1 = (f32[512,512]{1,0:T(8,128)S(1)}, f32[512,512]{1,0:T(8,128)S(1)}, f32[512,512]{1,0:T(8,128)S(1)}, f32[512,512]{1,0:T(8,128)S(1)}, f32[8192,1024]{1,0:T(8,128)S(1)}) custom-call(f32[512,512]{1,0:T(8,128)} %reduce.1.grad_in, f32[512,512]{1,0:T(8,128)} %bitcast.10, f32[512,512]{1,0:T(8,128)} %bitcast.11, f32[512,512]{1,0:T(8,128)} %bitcast.12, ...), custom_call_target="tpu_custom_call" | custom-call | tf_op jit(solution)/shard_map/gather/pallas_call | solution.py:533
  214.2 12.2 %flush.1 = (f32[512,512]{1,0:T(8,128)}, f32[512,512]{1,0:T(8,128)}, f32[512,512]{1,0:T(8,128)}, f32[512,512]{1,0:T(8,128)}, f32[1024,4096]{1,0:T(8,128)}, /*index=5*/f32[4096,1024]{1,0:T(8,128)}) custom-call(f32[512,512]{1,0:T(8,128)S(1)} %get-tuple-element.17.left, f32[512,512]{1,0:T(8,128)S(1)} %get-tuple-element.18.right, ...), custom_call_target="tpu_custom_call" | custom-call | tf_op jit(solution)/shard_map/flush/pallas_call | solution.py:558

commit v4 on v3

--- a/solution.py
+++ b/solution.py
@@ -19,7 +19,6 @@
 HOPS = (3, 2, 1, 0)
 PLANE = 208
 LINE = 512 - 2 * PLANE
-GATHER_HOPS = (0, 1, 3, 2)
 
 
 def dev(z, y, x, c):
@@ -380,12 +379,9 @@
 
 
 def gather_kernel(grad_in, rl_in, rr_in, sq_in, mom_in, sl_in, sr_in, w1_in, w2_in, new_left, new_right, new_sq, new_mom, w,
-                  buf, grad, rl, rr, pre, isem, zs, zr, xs, xr, ys, yr, xds, xdr, yds, ydr, cs, cr):
+                  buf, grad, rl, rr, pre, isem, zs, zr, xs, xr, ys, yr, xds, xdr, yds, ydr, cs, cr, ls, lr, lcs, lcr):
     z, y, x, c = coords()
     xp, yp, cp = dev(z, y, 1 - x, c), dev(z, 1 - y, x, c), dev(z, y, x, 1 - c)
-
-    def blk(zb, yb, xb, cb):
-        return dev(zb, yb, xb, cb)[0]
 
     pairs = [(grad_in, grad), (rl_in, rl), (rr_in, rr), (sq_in, new_sq), (mom_in, new_mom), (sl_in, new_left), (sr_in, new_right), (w2_in, w.at[pl.ds(4096, 4096)])]
     pairs += [(w1_in.at[:, pl.ds(1024 * n, 1024)], w.at[pl.ds(1024 * n, 1024)]) for n in range(4)]
@@ -394,7 +390,7 @@
         load.start()
     greet_signal(z, y, x, c)
 
-    b0 = blk(z, y, x, c)
+    own = y * 2 + x
     for load in loads[:4]:
         load.wait()
     for load in loads[5:]:
@@ -422,57 +418,111 @@
         r = strip_of(i)
         mom = MOM_DECAY * new_mom[r] + rl[r] * scale
         new_mom[r] = mom
-        buf[b0, r] = mom.astype(jnp.bfloat16)
+        buf[z, own, c, r] = mom.astype(jnp.bfloat16)
         return 0
 
     lax.fori_loop(0, 8, momentum_step, 0)
     greet_wait()
 
-    zb = [(z + 4 - h) % 4 for h in GATHER_HOPS]
-    spots = [(y, x), (1 - y, x), (y, 1 - x), (1 - y, 1 - x)]
-
-    def step(w, b, row, col):
+    low = z < 2
+    end = (z == 0) | (z == 3)
+    middle = jnp.logical_not(end)
+    near = [jnp.where(end, n, m) for n, m in ((1, 0), (2, 2), (3, 3))]
+    zb = [z] + [jnp.where(low, n, 3 - n) for n in near]
+    inner = dev(jnp.where(low, z + 1, z - 1), y, x, c)
+    outer = dev(jnp.where(low, 0, 3), y, x, c)
+    yx = [own, (1 - y) * 2 + x, y * 2 + 1 - x, (1 - y) * 2 + 1 - x]
+    line = pl.ds(2 * PLANE, LINE)
+
+    def step(zk, n, cb, first, count):
+        b = (zk * 4 + n) * 2 + cb
+        upper = zk < 2
+        col = jnp.where(upper, b % 8, b % 2)
+        row = jnp.where(upper, (col // 2) * 2 + b // 8, 8 + (b - 16) // 2)
+
         def strip(i, _):
-            r = pl.ds(pl.multiple_of(row * 512 + i * 64, 64), 64)
-            cc = pl.ds(pl.multiple_of(col * 512, 512), 512)
+            at = first + i * 32
+            r = pl.ds(pl.multiple_of(row * 512 + at, 32), 32)
+            cc = pl.ds(pl.multiple_of((col % 2) * 512, 512), 512)
             old = w[r, cc]
-            d = buf[b, pl.ds(pl.multiple_of(i * 64, 64), 64), :].astype(jnp.float32)
+            d = buf[zk, n, cb, pl.ds(pl.multiple_of(at, 32), 32), :].astype(jnp.float32)
             w[r, cc] = old - LEARN_RATE * (d + WEIGHT_DECAY * old)
             return 0
 
-        lax.fori_loop(0, 8, strip, 0)
-
-    def apply(b, zk):
-        first = zk < 2
-        col = jnp.where(first, b % 8, b % 2)
-        step(w, b, jnp.where(first, (col // 2) * 2 + b // 8, 8 + (b - 16) // 2), col % 2)
-
-    def part(ref, b, h):
-        return ref.at[b, pl.ds(h * 256, 256)]
-
-    def xcopy(k, b):
-        return remote(buf.at[b], buf.at[b], xs.at[k], xr.at[k], xp)
-
-    def ycopy(k, b):
-        return remote(buf.at[b], buf.at[b], ys.at[k], yr.at[k], yp)
-
-    def xdiag(k, b):
-        return remote(part(buf, b, 0), part(buf, b, 0), xds.at[k], xdr.at[k], xp)
-
-    def ydiag(k, b):
-        return remote(part(buf, b, 1), part(buf, b, 1), yds.at[k], ydr.at[k], yp)
-
-    def ccopy(k, i, b):
-        return remote(buf.at[b], buf.at[b], cs.at[k, i], cr.at[k, i], cp)
-
-    def zcopy(k, b, peer):
-        return remote(buf.at[b], buf.at[b], zs.at[k - 1], zr.at[k - 1], peer)
-
-    xcopy(0, b0).start()
-    ycopy(0, b0).start()
-    for k in (1, 2, 3):
-        zcopy(k, b0, dev((z + GATHER_HOPS[k]) % 4, y, x, c)).start()
-    ccopy(0, 0, b0).start()
+        lax.fori_loop(0, count, strip, 0)
+
+    def plane_rows(k):
+        return 512 if k == 0 else 2 * PLANE
+
+    def same(zk, n, where, ss, rs, peer):
+        ref = buf.at[zk, n, c, where]
+        return remote(ref, ref, ss, rs, peer)
+
+    def xcopy(k, n):
+        return same(zb[k], n, pl.ds(0, plane_rows(k)), xs.at[k], xr.at[k], xp)
+
+    def ycopy(k, n):
+        return same(zb[k], n, pl.ds(0, plane_rows(k)), ys.at[k], yr.at[k], yp)
+
+    def xdiag(k, n):
+        return same(zb[k], n, pl.ds(0, plane_rows(k) // 2), xds.at[k], xdr.at[k], xp)
+
+    def ydiag(k, n):
+        return same(zb[k], n, pl.ds(plane_rows(k) // 2, plane_rows(k) // 2), yds.at[k], ydr.at[k], yp)
+
+    def ccopy(k, i, n):
+        return same(zb[k], n, pl.ds(0, plane_rows(k)), cs.at[k, i], cr.at[k, i], cp)
+
+    def zcopy(layer, n, peer):
+        return same(layer, own, pl.ds(0, 2 * PLANE), zs.at[n], zr.at[layer], peer)
+
+    def zpass(k):
+        return zcopy(zb[k], k + 1, inner if k == 1 else outer)
+
+    def zown():
+        return zcopy(z, 0, inner), zcopy(z, 1, outer)
+
+    def lines(layer, ss, rs, peer):
+        ref = buf.at[layer, :, c, line]
+        return remote(ref, ref, ss, rs, peer)
+
+    def forward(k):
+        return lines(zb[k], ls.at[k + 1], lr.at[zb[k]], inner if k == 1 else outer)
+
+    def line_core(k):
+        return lines(zb[k], lcs.at[k - 1], lcr.at[k - 1], cp)
+
+    def start_line():
+        lines(z, ls.at[0], lr.at[z], inner).start()
+
+        @pl.when(middle)
+        def _():
+            lines(z, ls.at[1], lr.at[z], outer).start()
+
+    def take_line(k, where):
+        @pl.when(where)
+        def _():
+            forward(k).wait_recv()
+            if where is middle:
+                forward(k).start()
+            line_core(k).start()
+
+    def apply_line(k):
+        line_core(k).wait_recv()
+        for n in range(4):
+            for cb in range(2):
+                step(zb[k], n, cb, 2 * PLANE, LINE // 32)
+
+    xcopy(0, own).start()
+    ycopy(0, own).start()
+    to_inner, to_outer = zown()
+    to_inner.start()
+
+    @pl.when(middle)
+    def _():
+        to_outer.start()
+
+    ccopy(0, 0, own).start()
     for load in loads[5:7]:
         load.wait()
     pre[...] = mm(grad[...], grad[...], ((1,), (1,)))
@@ -487,41 +537,114 @@
     lax.fori_loop(0, 8, stats, 0)
     for load in loads[7:]:
         load.wait()
+
+    def meet(k):
+        ycopy(k, yx[1]).wait_recv()
+        xdiag(k, yx[1]).start()
+        ccopy(k, 1, yx[1]).start()
+        xcopy(k, yx[2]).wait_recv()
+        ydiag(k, yx[2]).start()
+        ccopy(k, 2, yx[2]).start()
+
+    def begin(k):
+        xcopy(k, own).start()
+        ycopy(k, own).start()
+        ccopy(k, 0, own).start()
+
+    def use(k):
+        for i in range(3):
+            step(zb[k], yx[i], c, 0, plane_rows(k) // 32)
+        for i in range(3):
+            ccopy(k, i, yx[i]).wait_recv()
+            step(zb[k], yx[i], 1 - c, 0, plane_rows(k) // 32)
+
+    def meet_last(k):
+        xdiag(k, yx[3]).wait_recv()
+        ydiag(k, yx[3]).wait_recv()
+        ccopy(k, 3, yx[3]).start()
+
+    def use_last(k):
+        step(zb[k], yx[3], c, 0, plane_rows(k) // 32)
+        ccopy(k, 3, yx[3]).wait_recv()
+        step(zb[k], yx[3], 1 - c, 0, plane_rows(k) // 32)
+
+    def pass_z(k):
+        zpass(k).wait_recv()
+        zpass(k).start()
+
+    meet(0)
+
+    @pl.when(end)
+    def _():
+        zpass(1).wait_recv()
+
+    @pl.when(middle)
+    def _():
+        pass_z(1)
+        pass_z(2)
+
+    begin(1)
+    use(0)
+    meet_last(0)
+    start_line()
+
+    @pl.when(end)
+    def _():
+        zpass(2).wait_recv()
+
+    @pl.when(middle)
+    def _():
+        pass_z(3)
+
+    begin(2)
+    use_last(0)
+    meet(1)
+    take_line(1, middle)
+
+    @pl.when(end)
+    def _():
+        zpass(3).wait_recv()
+
+    begin(3)
+    take_line(2, middle)
+    take_line(1, end)
+    use(1)
+    meet_last(1)
+    meet(2)
+    take_line(3, middle)
+    use_last(1)
+    apply_line(1)
+    use(2)
+    meet_last(2)
+    take_line(2, end)
+    use_last(2)
+    apply_line(2)
+    meet(3)
+    use(3)
+    take_line(3, end)
+    apply_line(3)
+    meet_last(3)
+    use_last(3)
+
     for k in range(4):
-        b, by, bx, bd = [blk(zb[k], yy, xx, c) for yy, xx in spots]
-        others = [blk(zb[k], yy, xx, 1 - c) for yy, xx in spots]
-        ycopy(k, by).wait_recv()
-        xdiag(k, by).start()
-        ccopy(k, 1, by).start()
-        xcopy(k, bx).wait_recv()
-        ydiag(k, bx).start()
-        ccopy(k, 2, bx).start()
-        if k < 3:
-            nb = blk(zb[k + 1], y, x, c)
-            zcopy(k + 1, nb, xp).wait_recv()
-            xcopy(k + 1, nb).start()
-            ycopy(k + 1, nb).start()
-            ccopy(k + 1, 0, nb).start()
-        for t in (b, by, bx):
-            apply(t, zb[k])
-        for i in range(3):
-            ccopy(k, i, others[i]).wait_recv()
-            apply(others[i], zb[k])
-        xdiag(k, bd).wait_recv()
-        ydiag(k, bd).wait_recv()
-        ccopy(k, 3, bd).start()
-        apply(bd, zb[k])
-        ccopy(k, 3, others[3]).wait_recv()
-        apply(others[3], zb[k])
-    for k in range(4):
-        xcopy(k, b0).wait_send()
-        ycopy(k, b0).wait_send()
-        xdiag(k, b0).wait_send()
-        ydiag(k, b0).wait_send()
+        xcopy(k, own).wait_send()
+        ycopy(k, own).wait_send()
+        xdiag(k, own).wait_send()
+        ydiag(k, own).wait_send()
         for i in range(4):
-            ccopy(k, i, b0).wait_send()
+            ccopy(k, i, own).wait_send()
         if k:
-            zcopy(k, b0, xp).wait_send()
+            line_core(k).wait_send()
+    to_inner.wait_send()
+    lines(z, ls.at[0], lr.at[z], inner).wait_send()
+
+    @pl.when(middle)
+    def _():
+        to_outer.wait_send()
+        lines(z, ls.at[1], lr.at[z], outer).wait_send()
+        for k in (1, 2, 3):
+            zpass(k).wait_send()
+            forward(k).wait_send()
 
 
 def finish_step(grad, root_left, root_right, graft_sq, momentum, stat_left, stat_right, w_fc1, w_fc2):
@@ -535,7 +658,7 @@
         out_shape=(tile, tile, tile, tile, pltpu.VMEM((8192, 1024), f32)),
         in_specs=[any_spec] * 9,
         out_specs=(vmem_spec,) * 5,
-        scratch_shapes=[pltpu.VMEM((32, 512, 512), bf)] + [pltpu.VMEM((512, 512), f32)] * 4 + [dma((12,)), dma((3,)), dma((3,))] + [dma((4,))] * 8 + [dma((4, 4)), dma((4, 4))],
+        scratch_shapes=[pltpu.VMEM((4, 4, 2, 512, 512), bf)] + [pltpu.VMEM((512, 512), f32)] * 4 + [dma((12,)), dma((5,)), dma((4,))] + [dma((4,))] * 8 + [dma((4, 4)), dma((4, 4)), dma((5,)), dma((4,)), dma((3,)), dma((3,))],
         compiler_params=pltpu.CompilerParams(collective_id=1, has_side_effects=True, vmem_limit_bytes=26 * 2 ** 20),
         name="gather",
     )(grad, root_left, root_right, graft_sq, momentum, stat_left, stat_right, w_fc1, w_fc2)

time: 227 us -> 220 us (0.969)
  Pallas kernels: 226 us -> 219 us
    pallas_call x1, Pallas kernels: 82.6 us -> 75.7 us  [finish_step(): pl.pallas_call(gather_kernel, out_shape=(tile, tile, tile, tile, pltpu.VM...]
where the time goes in v4:
time: 220 us
  Pallas kernels  219 us (100%)
    pallas_call x1, Pallas kernels, reduce_gradients(): pl.pallas_call(reduce_kernel, out_shape=jax.ShapeDtypeStruct((512, 512),...  131 us
    pallas_call x1, Pallas kernels, finish_step(): pl.pallas_call(gather_kernel, out_shape=(tile, tile, tile, tile, pltpu.VM...  75.7 us
    pallas_call x1, Pallas kernels, flush(): pl.pallas_call(flush_kernel, out_shape=(tile, tile, tile, tile, jax.Shape...  12.2 us

profile of v4, /device:TPU:0, one launch (start us, length us, event | category | flops | bytes accessed | tf_op | source)
XLA Modules:
  0.0 219.7 jit_solution(13338179871638070489)
XLA Ops:
  0.6 131.0 %reduce.1.grad_in = f32[512,512]{1,0:T(8,128)} custom-call(bf16[1024,1024]{1,0:T(8,128)(2,1)} %x_in.1, bf16[1024,4096]{1,0:T(8,128)(2,1)} %dy_mid.1, bf16[1024,4096]{1,0:T(8,128)(2,1)} %x_mid.1, bf16[1024,1024]{1,0:T(8,128)(2,1)} %dy_out.1), custom_call_target="tpu_custom_call" | custom-call | tf_op jit(solution)/shard_map/reduce/pallas_call | solution.py:363
  131.6 75.7 %gather.1 = (f32[512,512]{1,0:T(8,128)S(1)}, f32[512,512]{1,0:T(8,128)S(1)}, f32[512,512]{1,0:T(8,128)S(1)}, f32[512,512]{1,0:T(8,128)S(1)}, f32[8192,1024]{1,0:T(8,128)S(1)}) custom-call(f32[512,512]{1,0:T(8,128)} %reduce.1.grad_in, f32[512,512]{1,0:T(8,128)} %bitcast.10, f32[512,512]{1,0:T(8,128)} %bitcast.11, f32[512,512]{1,0:T(8,128)} %bitcast.12, ...), custom_call_target="tpu_custom_call" | custom-call | tf_op jit(solution)/shard_map/gather/pallas_call | solution.py:656
  207.3 12.2 %flush.1 = (f32[512,512]{1,0:T(8,128)}, f32[512,512]{1,0:T(8,128)}, f32[512,512]{1,0:T(8,128)}, f32[512,512]{1,0:T(8,128)}, f32[1024,4096]{1,0:T(8,128)}, /*index=5*/f32[4096,1024]{1,0:T(8,128)}) custom-call(f32[512,512]{1,0:T(8,128)S(1)} %get-tuple-element.17.left, f32[512,512]{1,0:T(8,128)S(1)} %get-tuple-element.18.right, ...), custom_call_target="tpu_custom_call" | custom-call | tf_op jit(solution)/shard_map/flush/pallas_call | solution.py:681

commit v5 on v4

--- a/solution.py
+++ b/solution.py
@@ -19,6 +19,8 @@
 HOPS = (3, 2, 1, 0)
 PLANE = 208
 LINE = 512 - 2 * PLANE
+GATHER_PLANE = 208
+GATHER_LINE = 512 - 2 * GATHER_PLANE
 
 
 def dev(z, y, x, c):
@@ -395,21 +397,23 @@
         load.wait()
     for load in loads[5:]:
         load.start()
-    pre[...] = mm(rl[...], grad[...])
-    rl[...] = mm(pre[...], rr[...])
+    pre[...] = mm3(rl[...], grad[...])
+    rl[...] = mm3(pre[...], rr[...])
 
     def strip_of(i):
         return pl.ds(pl.multiple_of(i * 64, 64), 64)
 
     def norms(i, sums):
-        r = strip_of(i)
+        r = pl.ds(pl.multiple_of(i * 16, 16), 16)
         g, p = grad[r], rl[r]
         sq = STAT_DECAY * new_sq[r] + (1.0 - STAT_DECAY) * g * g
         new_sq[r] = sq
         h = g / (jnp.sqrt(sq / BIAS_CORR) + GRAFT_EPS)
-        return sums[0] + jnp.sum(h * h), sums[1] + jnp.sum(p * p)
-
-    graft_sum, pre_sum = lax.fori_loop(0, 8, norms, (jnp.float32(0.0), jnp.float32(0.0)))
+        return sums[0] + h * h, sums[1] + p * p
+
+    zero = jnp.zeros((16, 512), jnp.float32)
+    graft_sq_sum, pre_sq_sum = lax.fori_loop(0, 32, norms, (zero, zero))
+    graft_sum, pre_sum = jnp.sum(graft_sq_sum), jnp.sum(pre_sq_sum)
     loads[4].wait()
     ones = jnp.ones((64, 512), jnp.float32)
     scale = jnp.sqrt(graft_sum * ones) / jnp.sqrt(pre_sum * ones)
@@ -432,7 +436,7 @@
     inner = dev(jnp.where(low, z + 1, z - 1), y, x, c)
     outer = dev(jnp.where(low, 0, 3), y, x, c)
     yx = [own, (1 - y) * 2 + x, y * 2 + 1 - x, (1 - y) * 2 + 1 - x]
-    line = pl.ds(2 * PLANE, LINE)
+    line = pl.ds(2 * GATHER_PLANE, GATHER_LINE)
 
     def step(zk, n, cb, first, count):
         b = (zk * 4 + n) * 2 + cb
@@ -452,17 +456,28 @@
         lax.fori_loop(0, count, strip, 0)
 
     def plane_rows(k):
-        return 512 if k == 0 else 2 * PLANE
+        return 512 if k == 0 else 2 * GATHER_PLANE
 
     def same(zk, n, where, ss, rs, peer):
         ref = buf.at[zk, n, c, where]
         return remote(ref, ref, ss, rs, peer)
 
+    def halves(k, n, sems, peer):
+        rows = plane_rows(k) // 2
+        return [same(zb[k], n, pl.ds(h * rows, rows), sems[0].at[k, h], sems[1].at[k, h], peer) for h in range(2)]
+
     def xcopy(k, n):
-        return same(zb[k], n, pl.ds(0, plane_rows(k)), xs.at[k], xr.at[k], xp)
+        return halves(k, n, (xs, xr), xp)
 
     def ycopy(k, n):
-        return same(zb[k], n, pl.ds(0, plane_rows(k)), ys.at[k], yr.at[k], yp)
+        return halves(k, n, (ys, yr), yp)
+
+    def send_plane(k):
+        across, down = xcopy(k, own), ycopy(k, own)
+        across[1].start()
+        down[0].start()
+        across[0].start()
+        down[1].start()
 
     def xdiag(k, n):
         return same(zb[k], n, pl.ds(0, plane_rows(k) // 2), xds.at[k], xdr.at[k], xp)
@@ -474,7 +489,7 @@
         return same(zb[k], n, pl.ds(0, plane_rows(k)), cs.at[k, i], cr.at[k, i], cp)
 
     def zcopy(layer, n, peer):
-        return same(layer, own, pl.ds(0, 2 * PLANE), zs.at[n], zr.at[layer], peer)
+        return same(layer, own, pl.ds(0, 2 * GATHER_PLANE), zs.at[n], zr.at[layer], peer)
 
     def zpass(k):
         return zcopy(zb[k], k + 1, inner if k == 1 else outer)
@@ -511,10 +526,9 @@
         line_core(k).wait_recv()
         for n in range(4):
             for cb in range(2):
-                step(zb[k], n, cb, 2 * PLANE, LINE // 32)
-
-    xcopy(0, own).start()
-    ycopy(0, own).start()
+                step(zb[k], n, cb, 2 * GATHER_PLANE, GATHER_LINE // 32)
+
+    send_plane(0)
     to_inner, to_outer = zown()
     to_inner.start()
 
@@ -539,16 +553,18 @@
         load.wait()
 
     def meet(k):
-        ycopy(k, yx[1]).wait_recv()
+        down, across = ycopy(k, yx[1]), xcopy(k, yx[2])
+        down[0].wait_recv()
         xdiag(k, yx[1]).start()
+        across[1].wait_recv()
+        ydiag(k, yx[2]).start()
+        down[1].wait_recv()
         ccopy(k, 1, yx[1]).start()
-        xcopy(k, yx[2]).wait_recv()
-        ydiag(k, yx[2]).start()
+        across[0].wait_recv()
         ccopy(k, 2, yx[2]).start()
 
     def begin(k):
-        xcopy(k, own).start()
-        ycopy(k, own).start()
+        send_plane(k)
         ccopy(k, 0, own).start()
 
     def use(k):
@@ -627,8 +643,8 @@
     use_last(3)
 
     for k in range(4):
-        xcopy(k, own).wait_send()
-        ycopy(k, own).wait_send()
+        for sent in xcopy(k, own) + ycopy(k, own):
+            sent.wait_send()
         xdiag(k, own).wait_send()
         ydiag(k, own).wait_send()
         for i in range(4):
@@ -658,7 +674,7 @@
         out_shape=(tile, tile, tile, tile, pltpu.VMEM((8192, 1024), f32)),
         in_specs=[any_spec] * 9,
         out_specs=(vmem_spec,) * 5,
-        scratch_shapes=[pltpu.VMEM((4, 4, 2, 512, 512), bf)] + [pltpu.VMEM((512, 512), f32)] * 4 + [dma((12,)), dma((5,)), dma((4,))] + [dma((4,))] * 8 + [dma((4, 4)), dma((4, 4)), dma((5,)), dma((4,)), dma((3,)), dma((3,))],
+        scratch_shapes=[pltpu.VMEM((4, 4, 2, 512, 512), bf)] + [pltpu.VMEM((512, 512), f32)] * 4 + [dma((12,)), dma((5,)), dma((4,))] + [dma((4, 2))] * 4 + [dma((4,))] * 4 + [dma((4, 4)), dma((4, 4)), dma((5,)), dma((4,)), dma((3,)), dma((3,))],
         compiler_params=pltpu.CompilerParams(collective_id=1, has_side_effects=True, vmem_limit_bytes=26 * 2 ** 20),
         name="gather",
     )(grad, root_left, root_right, graft_sq, momentum, stat_left, stat_right, w_fc1, w_fc2)
@@ -689,6 +705,14 @@
     )(*values)
 
 
+def mm3(a, b):
+    a_high, b_high = a.astype(jnp.bfloat16), b.astype(jnp.bfloat16)
+    a_low = (a - a_high.astype(jnp.float32)).astype(jnp.bfloat16)
+    b_low = (b - b_high.astype(jnp.float32)).astype(jnp.bfloat16)
+    parts = [jnp.dot(p, q, preferred_element_type=jnp.float32) for p, q in ((a_high, b_low), (a_low, b_high), (a_high, b_high))]
+    return parts[0] + parts[1] + parts[2]
+
+
 def mm(a, b, dims=((1,), (0,))):
     return lax.dot_general(a, b, (dims, ((), ())), precision=lax.Precision.HIGHEST, preferred_element_type=jnp.float32)
 

time: 220 us -> 216 us (0.982)
  Pallas kernels: 219 us -> 215 us
    pallas_call x1, Pallas kernels: 75.7 us -> 71.6 us  [finish_step(): pl.pallas_call(gather_kernel, out_shape=(tile, tile, tile, tile, pltpu.VM...]
where the time goes in v5:
time: 216 us
  Pallas kernels  215 us (100%)
    pallas_call x1, Pallas kernels, reduce_gradients(): pl.pallas_call(reduce_kernel, out_shape=jax.ShapeDtypeStruct((512, 512),...  131 us
    pallas_call x1, Pallas kernels, finish_step(): pl.pallas_call(gather_kernel, out_shape=(tile, tile, tile, tile, pltpu.VM...  71.6 us
    pallas_call x1, Pallas kernels, flush(): pl.pallas_call(flush_kernel, out_shape=(tile, tile, tile, tile, jax.Shape...  12.2 us

profile of v5, /device:TPU:0, one launch (start us, length us, event | category | flops | bytes accessed | tf_op | source)
XLA Modules:
  0.0 215.6 jit_solution(9799122784168910431)
XLA Ops:
  0.6 131.0 %reduce.1.grad_in = f32[512,512]{1,0:T(8,128)} custom-call(bf16[1024,1024]{1,0:T(8,128)(2,1)} %x_in.1, bf16[1024,4096]{1,0:T(8,128)(2,1)} %dy_mid.1, bf16[1024,4096]{1,0:T(8,128)(2,1)} %x_mid.1, bf16[1024,1024]{1,0:T(8,128)(2,1)} %dy_out.1), custom_call_target="tpu_custom_call" | custom-call | tf_op jit(solution)/shard_map/reduce/pallas_call | solution.py:365
  131.6 71.6 %gather.1 = (f32[512,512]{1,0:T(8,128)S(1)}, f32[512,512]{1,0:T(8,128)S(1)}, f32[512,512]{1,0:T(8,128)S(1)}, f32[512,512]{1,0:T(8,128)S(1)}, f32[8192,1024]{1,0:T(8,128)S(1)}) custom-call(f32[512,512]{1,0:T(8,128)} %reduce.1.grad_in, f32[512,512]{1,0:T(8,128)} %bitcast.10, f32[512,512]{1,0:T(8,128)} %bitcast.11, f32[512,512]{1,0:T(8,128)} %bitcast.12, ...), custom_call_target="tpu_custom_call" | custom-call | tf_op jit(solution)/shard_map/gather/pallas_call | solution.py:672
  203.2 12.2 %flush.1 = (f32[512,512]{1,0:T(8,128)}, f32[512,512]{1,0:T(8,128)}, f32[512,512]{1,0:T(8,128)}, f32[512,512]{1,0:T(8,128)}, f32[1024,4096]{1,0:T(8,128)}, /*index=5*/f32[4096,1024]{1,0:T(8,128)}) custom-call(f32[512,512]{1,0:T(8,128)S(1)} %get-tuple-element.17.left, f32[512,512]{1,0:T(8,128)S(1)} %get-tuple-element.18.right, ...), custom_call_target="tpu_custom_call" | custom-call | tf_op jit(solution)/shard_map/flush/pallas_call | solution.py:697
